TPU v7x, 32 devices: a 4x2x2 block of a 4x4x8 slice. The times are simulated.
32 devices in a mesh: dp: 4 (over y, z), ep: 8 (over x, core).
Axes of the slice: x: 4, y: 2, z: 2, core: 2. Of those that a mesh axis runs over, the one named last changes fastest.
The devices are a block of a 4x4x8 slice.
Arguments:
- x_tokens: bfloat16 [4096, 1024], P(('dp', 'ep')), parts along dimension 0
- dy_tokens: bfloat16 [4096, 1024], P(('dp', 'ep')), parts along dimension 0
- expert_ids: int32 [4096, 8], P(('dp', 'ep')), parts along dimension 0
- gate_vals: float32 [4096, 8], P(('dp', 'ep')), parts along dimension 0
- slot_ids: int32 [4096, 8], P(('dp', 'ep')), parts along dimension 0
- w_gate: bfloat16 [32, 1024, 512], P('ep')
- w_down: bfloat16 [32, 512, 1024], P('ep')
- w_up: bfloat16 [32, 1024, 512], P('ep')
Outputs:
- output 1: bfloat16 [4096, 1024], P(('dp', 'ep')), parts along dimension 0
- output 2: float32 [128, 1024, 512], P(('dp', 'ep')), parts along dimension 0
- output 3: float32 [128, 512, 1024], P(('dp', 'ep')), parts along dimension 0
- output 4: float32 [128, 1024, 512], P(('dp', 'ep')), parts along dimension 0
There are 4 independent parts. A program takes and returns all parts, laid end to end along the dimension named above; an argument that names none is the same for every part.
All inputs are finite; a program needn't handle non-finite values.
Results may differ from a plain program's by a relative error of at most 0.0103867.
Values are sent between devices in bfloat16 or wider.
A program may use at most 768 MiB of HBM per device.

v0:
```python
import jax
import jax.numpy as jnp
from jax import lax
from jax.sharding import PartitionSpec as P


def slot_capacity(tok_dev, top_k, n_exp):
    return ((3 * tok_dev * top_k) // (2 * n_exp) + 7) // 8 * 8


def source_dispatch(x_src, dy_src, ids_src, gate_src, slot_src, cap_rows, n_exp):
    tok_dev, top_k = ids_src.shape
    n_copy = tok_dev * top_k
    d_model = x_src.shape[1]
    flat_slot = jnp.where(slot_src >= 0, ids_src * cap_rows + slot_src, n_exp * cap_rows)
    slot_copy = jnp.full((n_exp * cap_rows,), n_copy, jnp.int32).at[flat_slot.reshape(n_copy)].set(jnp.arange(n_copy, dtype=jnp.int32), mode='drop')
    slot_tok = slot_copy // top_k
    x_send = jnp.take(x_src, slot_tok, axis=0, mode='fill', fill_value=0)
    dy_send = jnp.take(dy_src, slot_tok, axis=0, mode='fill', fill_value=0)
    gate_slot = jnp.take(gate_src.reshape(n_copy), slot_copy, mode='fill', fill_value=0)
    dz_send = (gate_slot[:, None] * dy_send).astype(jnp.bfloat16)
    return x_send.reshape(n_exp, cap_rows, d_model), dz_send.reshape(n_exp, cap_rows, d_model), flat_slot


def source_combine(dx_send, flat_slot):
    n_exp, cap_rows, d_model = dx_send.shape
    rows = jnp.take(dx_send.reshape(n_exp * cap_rows, d_model), flat_slot, axis=0, mode='fill', fill_value=0)
    return jnp.sum(rows, axis=1, dtype=jnp.float32).astype(jnp.bfloat16)


def expert_backward(x_rows, dz_rows, w_gate, w_down, w_up):
    a_pre = jnp.einsum('erd,edf->erf', x_rows, w_gate, preferred_element_type=jnp.float32).astype(jnp.bfloat16).astype(jnp.float32)
    b_pre = jnp.einsum('erd,edf->erf', x_rows, w_up, preferred_element_type=jnp.float32).astype(jnp.bfloat16).astype(jnp.float32)
    sigma_a = jax.nn.sigmoid(a_pre)
    silu_a = a_pre * sigma_a
    hidden = (silu_a * b_pre).astype(jnp.bfloat16)
    d_hidden = jnp.einsum('erd,efd->erf', dz_rows, w_down, preferred_element_type=jnp.float32)
    d_gate = (d_hidden * b_pre * sigma_a * (1.0 + a_pre * (1.0 - sigma_a))).astype(jnp.bfloat16)
    d_up = (d_hidden * silu_a).astype(jnp.bfloat16)
    g_down = jnp.einsum('erf,erd->efd', hidden, dz_rows, preferred_element_type=jnp.float32)
    g_gate = jnp.einsum('erd,erf->edf', x_rows, d_gate, preferred_element_type=jnp.float32)
    g_up = jnp.einsum('erd,erf->edf', x_rows, d_up, preferred_element_type=jnp.float32)
    dx_rows = (jnp.einsum('erf,edf->erd', d_gate, w_gate, preferred_element_type=jnp.float32) + jnp.einsum('erf,edf->erd', d_up, w_up, preferred_element_type=jnp.float32)).astype(jnp.bfloat16)
    return dx_rows, g_gate, g_down, g_up


def solution(mesh):
    n_dev = mesh.shape['ep']

    def local_step(x_loc, dy_loc, ids_loc, gate_loc, slot_loc, w_gate, w_down, w_up):
        tok_dev, top_k = ids_loc.shape
        n_local = w_gate.shape[0]
        n_exp = n_local * n_dev
        d_model = x_loc.shape[1]
        cap_rows = slot_capacity(tok_dev, top_k, n_exp)
        x_send, dz_send, flat_slot = source_dispatch(x_loc, dy_loc, ids_loc, gate_loc, slot_loc, cap_rows, n_exp)
        x_recv = lax.all_to_all(x_send.reshape(n_exp, 1, cap_rows, d_model), 'ep', 0, 1, tiled=True)
        dz_recv = lax.all_to_all(dz_send.reshape(n_exp, 1, cap_rows, d_model), 'ep', 0, 1, tiled=True)
        dx_rows, g_gate, g_down, g_up = expert_backward(x_recv.reshape(n_local, n_dev * cap_rows, d_model), dz_recv.reshape(n_local, n_dev * cap_rows, d_model), w_gate, w_down, w_up)
        dx_back = lax.all_to_all(dx_rows.reshape(n_local, n_dev, cap_rows, d_model), 'ep', 1, 0, tiled=True)
        dx_loc = source_combine(dx_back.reshape(n_exp, cap_rows, d_model), flat_slot)
        return dx_loc, g_gate, g_down, g_up

    tok_spec = P(('dp', 'ep'), None)
    w_spec = P('ep', None, None)
    grad_spec = P(('dp', 'ep'), None, None)
    return jax.shard_map(local_step, mesh=mesh, in_specs=(tok_spec, tok_spec, tok_spec, tok_spec, tok_spec, w_spec, w_spec, w_spec), out_specs=(tok_spec, grad_spec, grad_spec, grad_spec), check_vma=False)
```

profile of v0, /device:TPU:81, one launch (start us, length us, event | category | flops | bytes accessed | tf_op | source)
XLA Modules:
  0.0 166.3 jit_solution(9995325965725974341)
XLA Ops:
  0.6 0.0 copy-start
  0.6 0.8 compare_and_fusion.1
  1.4 0.1 copy.28
  1.5 0.1 reshape.71
  1.6 4.3 %scatter_custom_fusion = s32[1536]{0:T(1024)S(1)} fusion(s32[1024]{0:T(1024)S(1)} %bitcast.50, s32[1024]{0:T(1024)S(1)} %iota.3, s32[]{:T(128)} %constant.58.clone.1), kind=kCustom, calls=%fused_computation.42 | custom fusion | bytes 6148 | tf_op jit(solution)/shard_map/scatter | solution.py:16
  6.0 0.0 copy-done
  6.0 5.1 %gather_fusion.3 = bf16[1536,1024]{1,0:T(8,128)(2,1)S(1)} fusion(bf16[128,1024]{1,0:T(8,128)(2,1)S(1)} %copy-done, s32[2048]{0:T(1024)S(1)} %pad_clamp_fusion), kind=kCustom, calls=%fused_computation.1.clone | custom fusion | bytes 6297600 | tf_op jit(solution)/shard_map/jit(_take)/gather | solution.py:18
  11.1 2.1 %broadcast_select_fusion = bf16[1536,1024]{1,0:T(8,128)(2,1)} fusion(bf16[1536,1024]{1,0:T(8,128)(2,1)S(1)} %gather_fusion.3, pred[1536]{0:T(1024)(128)(4,1)S(1)} %get-tuple-element.7), kind=kLoop, calls=%fused_computation.21 | loop fusion | flops 1572864 | bytes 6292992 | tf_op jit(solution)/shard_map/jit(_take)/select_n | solution.py:18
  13.2 0.0 copy-start.10
  13.2 0.0 copy-start.2
  13.2 6.1 %all-to-all-start.1 = ((bf16[32,1,48,1024]{3,2,1,0:T(8,128)(2,1)}), bf16[32,1,48,1024]{3,2,1,0:T(8,128)(2,1)S(1)}, u32[]{:S(2)}, u32[]{:S(2)}) async-start(bf16[32,1,48,1024]{3,2,1,0:T(8,128)(2,1)} %bitcast.45), calls=%async_computation.1 | async-start | bytes 6291456 | tf_op jit(solution)/shard_map/all_to_all | solution.py:57
  19.3 0.0 copy-done.10
  19.3 0.1 copy.29
  19.4 0.1 reshape.72
  19.5 0.0 copy-done.2
  19.5 5.8 %gather_fusion.2 = bf16[1536,1024]{1,0:T(8,128)(2,1)} fusion(bf16[128,1024]{1,0:T(8,128)(2,1)S(1)} %copy-done.2, s32[2048]{0:T(1024)S(1)} %pad_clamp_fusion), kind=kCustom, calls=%fused_computation.clone | custom fusion | bytes 6297600 | tf_op jit(solution)/shard_map/jit(_take)/gather | solution.py:19
  25.3 5.8 %gather_fusion = f32[1536]{0:T(1024)S(1)} fusion(f32[1024]{0:T(1024)S(1)} %reshape.72, s32[2048]{0:T(1024)S(1)} %pad_clamp_fusion.1), kind=kCustom, calls=%fused_computation.2 | custom fusion | bytes 18432 | tf_op jit(solution)/shard_map/jit(_take)/gather | solution.py:20
  31.2 3.7 %multiply_convert_fusion = bf16[1536,1024]{1,0:T(8,128)(2,1)} fusion(bf16[1536,1024]{1,0:T(8,128)(2,1)} %gather_fusion.2, f32[1536]{0:T(1024)S(1)} %and_select_fusion, pred[1536]{0:T(1024)(128)(4,1)S(1)} %get-tuple-element.7), kind=kLoop, calls=%fused_computation.6 | loop fusion | flops 6291456 | bytes 6299136 | tf_op jit(solution)/shard_map/convert_element_type | solution.py:21
  34.9 21.7 %all-to-all-done.1 = bf16[32,1,48,1024]{3,2,1,0:T(8,128)(2,1)S(1)} async-done(((bf16[32,1,48,1024]{3,2,1,0:T(8,128)(2,1)}), bf16[32,1,48,1024]{3,2,1,0:T(8,128)(2,1)S(1)}, u32[]{:S(2)}, u32[]{:S(2)}) %all-to-all-start.1) | async-done | bytes 3145760 | tf_op jit(solution)/shard_map/all_to_all | solution.py:57
  56.6 5.5 %all-to-all-start = ((bf16[32,1,48,1024]{3,2,1,0:T(8,128)(2,1)}), bf16[32,1,48,1024]{3,2,1,0:T(8,128)(2,1)}, u32[]{:S(2)}, u32[]{:S(2)}) async-start(bf16[32,1,48,1024]{3,2,1,0:T(8,128)(2,1)} %bitcast.46), calls=%async_computation | async-start | bytes 6291456 | tf_op jit(solution)/shard_map/all_to_all | solution.py:58
  62.1 0.0 copy-start.6
  62.1 0.4 copy.33
  62.5 0.0 copy-start.3
  62.5 2.9 %copy-done.6 = bf16[4,1024,512]{2,1,0:T(8,128)(2,1)S(1)} copy-done((bf16[4,1024,512]{2,1,0:T(8,128)(2,1)S(1)}, bf16[4,1024,512]{2,1,0:T(8,128)(2,1)}, u32[]{:S(2)}) %copy-start.6) | copy-done | bytes 4194328
  65.4 1.8 %convolution_convert_fusion = bf16[4,384,512]{2,1,0:T(8,128)(2,1)S(1)} fusion(bf16[4,384,1024]{2,1,0:T(8,128)(2,1)S(1)} %bitcast.40, bf16[4,1024,512]{2,1,0:T(8,128)(2,1)S(1)} %copy-done.6), kind=kOutput, calls=%fused_computation.24 | convolution fusion | flops 1611399168 | bytes 8912896 | tf_op jit(solution)/shard_map/erd,edf->erf/dot_general | solution.py:32
  67.2 0.0 copy-done.3
  67.2 0.4 copy-done.12
  67.6 1.8 %convolution_convert_fusion.1 = bf16[4,384,512]{2,1,0:T(8,128)(2,1)S(1)} fusion(bf16[4,384,1024]{2,1,0:T(8,128)(2,1)S(1)} %bitcast.41, bf16[4,1024,512]{2,1,0:T(8,128)(2,1)S(1)} %copy-done.12), kind=kOutput, calls=%fused_computation.25 | convolution fusion | flops 1611399168 | bytes 8912896 | tf_op jit(solution)/shard_map/erd,edf->erf/dot_general | solution.py:33
  69.4 0.0 copy-start.16
  69.4 30.1 %all-to-all-done = bf16[32,1,48,1024]{3,2,1,0:T(8,128)(2,1)} async-done(((bf16[32,1,48,1024]{3,2,1,0:T(8,128)(2,1)}), bf16[32,1,48,1024]{3,2,1,0:T(8,128)(2,1)}, u32[]{:S(2)}, u32[]{:S(2)}) %all-to-all-start) | async-done | bytes 3145760 | tf_op jit(solution)/shard_map/all_to_all | solution.py:58
  99.5 2.4 %copy.31 = bf16[4,8,1,48,1024]{4,3,1,0,2:T(8,128)(2,1)S(1)} copy(bf16[4,8,1,48,1024]{4,3,0,1,2:T(8,128)(2,1)} %bitcast.4) | data formatting | bytes 6291456 | tf_op jit(solution)/shard_map/all_to_all | solution.py:58
  101.9 0.0 copy-start.8
  101.9 0.0 copy-done.16
  101.9 0.7 copy-done.11
  102.7 4.3 %fusion.2 = (bf16[4,384,512]{2,1,0:T(8,128)(2,1)S(1)}, f32[4,384,512]{2,1,0:T(8,128)}) fusion(bf16[4,384,512]{2,1,0:T(8,128)(2,1)S(1)} %convolution_convert_fusion.1, bf16[4,384,512]{2,1,0:T(8,128)(2,1)S(1)} %convolution_convert_fusion, bf16[4,384,1024]{2,1,0:T(8,128)(2,1)S(1)} %bitcast.47, bf16[4,512,1024]{2,1,0:T(8,128)(2,1)S(1)} %copy-done.11), kind=kOutput, calls=%fused_computation.14 | convolution fusion | flops 1620049920 | bytes 15204352 | tf_op jit(solution)/shard_map/erd,efd->erf/dot_general | solution.py:37
  107.0 0.0 copy-done.8
  107.0 0.0 copy-done.7
  107.0 1.8 %fusion.17 = f32[4,384,1024]{2,1,0:T(8,128)S(1)} fusion(bf16[4,384,512]{2,1,0:T(8,128)(2,1)S(1)} %get-tuple-element.9, bf16[4,1024,512]{2,1,0:T(8,128)(2,1)S(1)} %copy-done.7), kind=kOutput, calls=%fused_computation.49 | convolution fusion | flops 1610612736 | bytes 12058624 | tf_op jit(solution)/shard_map/erf,edf->erd/dot_general | solution.py:43
  108.8 0.0 copy-done.5
  108.8 0.0 copy-done.14
  108.8 0.9 copy-done.13
  109.7 3.9 %add_convert_fusion = bf16[4,384,1024]{2,1,0:T(8,128)(2,1)S(1)} fusion(f32[4,384,1024]{2,1,0:T(8,128)S(1)} %fusion.17, bf16[4,1024,512]{2,1,0:T(8,128)(2,1)S(1)} %copy-done.13, f32[4,384,512]{2,1,0:T(8,128)} %get-tuple-element.10, bf16[4,384,512]{2,1,0:T(8,128)(2,1)S(1)} %convolution_convert_fusion), kind=kOutput, calls=%fused_computation.5 | convolution fusion | flops 1619263488 | bytes 18350080 | tf_op jit(solution)/shard_map/erf,edf->erd/dot_general | solution.py:43
  113.7 2.0 %copy.34 = bf16[4,8,48,1024]{3,2,0,1:T(8,128)(2,1)} copy(bf16[4,8,48,1024]{3,2,1,0:T(8,128)(2,1)S(1)} %bitcast.49) | data formatting | bytes 6291456 | tf_op jit(solution)/shard_map/reshape | solution.py:60
  115.6 4.6 %all-to-all-start.2 = ((bf16[4,8,48,1024]{3,2,0,1:T(8,128)(2,1)}), bf16[4,8,48,1024]{3,2,0,1:T(8,128)(2,1)S(1)}, u32[]{:S(2)}, u32[]{:S(2)}) async-start(bf16[4,8,48,1024]{3,2,0,1:T(8,128)(2,1)} %copy.34), calls=%async_computation.2 | async-start | bytes 6291456 | tf_op jit(solution)/shard_map/all_to_all | solution.py:60
  120.3 0.1 copy.27
  120.4 0.1 copy.35
  120.5 0.1 reshape.102
  120.6 0.0 copy-start.9
  120.6 0.0 copy-start.15
  120.6 0.0 copy-start.17
  120.6 8.3 %fusion.18 = f32[4,1024,512]{2,1,0:T(8,128)} fusion(bf16[4,384,1024]{2,1,0:T(8,128)(2,1)} %bitcast.42, bf16[4,384,512]{2,1,0:T(8,128)(2,1)} %copy-done.5), kind=kOutput, calls=%fused_computation.50 | convolution fusion | flops 1610612736 | bytes 13107200 | tf_op jit(solution)/shard_map/erd,erf->edf/dot_general | solution.py:41
  128.9 0.0 copy-done.9
  128.9 0.0 copy-done.15
  128.9 0.0 copy-done.17
  128.9 0.0 copy-start.4
  128.9 0.0 copy-start.18
  129.0 6.0 %fusion.9 = f32[4,512,1024]{2,1,0:T(8,128)} fusion(bf16[4,384,1024]{2,1,0:T(8,128)(2,1)S(1)} %bitcast.48, bf16[4,384,512]{2,1,0:T(8,128)(2,1)S(1)} %copy-done.17, bf16[4,384,512]{2,1,0:T(8,128)(2,1)S(1)} %copy-done.15), kind=kOutput, calls=%fused_computation.26 | convolution fusion | flops 1616904192 | bytes 14680064 | tf_op jit(solution)/shard_map/erf,erd->efd/dot_general | solution.py:40
  134.9 0.0 copy-done.4
  134.9 0.0 copy-done.18
  134.9 5.9 %fusion.16 = f32[4,1024,512]{2,1,0:T(8,128)} fusion(bf16[4,384,1024]{2,1,0:T(8,128)(2,1)S(1)} %bitcast.43, f32[4,384,512]{2,1,0:T(8,128)S(1)} %copy-done.18, bf16[4,384,512]{2,1,0:T(8,128)(2,1)S(1)} %copy-done.15), kind=kOutput, calls=%fused_computation.48 | convolution fusion | flops 1616117760 | bytes 16252928 | tf_op jit(solution)/shard_map/erd,erf->edf/dot_general | solution.py:42
  140.8 16.8 %all-to-all-done.2 = bf16[4,8,48,1024]{3,2,0,1:T(8,128)(2,1)S(1)} async-done(((bf16[4,8,48,1024]{3,2,0,1:T(8,128)(2,1)}), bf16[4,8,48,1024]{3,2,0,1:T(8,128)(2,1)S(1)}, u32[]{:S(2)}, u32[]{:S(2)}) %all-to-all-start.2) | async-done | bytes 3145760 | tf_op jit(solution)/shard_map/all_to_all | solution.py:60
  157.6 5.3 %gather_fusion.1 = bf16[1024,1024]{1,0:T(8,128)(2,1)} fusion(bf16[1536,1024]{1,0:T(8,128)(2,1)S(1)} %bitcast.39, s32[1024]{0:T(1024)S(1)} %broadcast_clamp_fusion), kind=kCustom, calls=%fused_computation.3 | custom fusion | bytes 4198400 | tf_op jit(solution)/shard_map/jit(_take)/gather | solution.py:27
  162.9 3.4 %fusion.8 = bf16[128,1024]{1,0:T(8,128)(2,1)} fusion(bf16[1024,1024]{1,0:T(8,128)(2,1)} %gather_fusion.1, pred[128,8]{1,0:T(8,128)(4,1)S(1)} %copy.27), kind=kLoop, calls=%fused_computation.23 | loop fusion | flops 1966080 | bytes 2360320 | tf_op jit(solution)/shard_map/reduce_sum | solution.py:28
  166.3 0.0 copy-done.1
  (16 shorter events, 0.1 us)
Async XLA Ops:
  0.6 5.4 %copy-start = (bf16[128,1024]{1,0:T(8,128)(2,1)S(1)}, bf16[128,1024]{1,0:T(8,128)(2,1)}, u32[]{:S(2)}) copy-start(bf16[128,1024]{1,0:T(8,128)(2,1)} %param.10) | copy-start | bytes 786436
  13.2 6.2 %copy-start.10 = (f32[128,8]{0,1:T(8,128)S(1)}, f32[128,8]{0,1:T(8,128)}, u32[]{:S(2)}) copy-start(f32[128,8]{0,1:T(8,128)} %param.13) | copy-start | bytes 12292
  13.2 6.3 %copy-start.2 = (bf16[128,1024]{1,0:T(8,128)(2,1)S(1)}, bf16[128,1024]{1,0:T(8,128)(2,1)}, u32[]{:S(2)}) copy-start(bf16[128,1024]{1,0:T(8,128)(2,1)} %param.11) | copy-start | bytes 786436
  13.2 43.4 %all-to-all-start.1 = ((bf16[32,1,48,1024]{3,2,1,0:T(8,128)(2,1)}), bf16[32,1,48,1024]{3,2,1,0:T(8,128)(2,1)S(1)}, u32[]{:S(2)}, u32[]{:S(2)}) async-start(bf16[32,1,48,1024]{3,2,1,0:T(8,128)(2,1)} %bitcast.45), calls=%async_computation.1 | async-start | bytes 6291456 | tf_op jit(solution)/shard_map/all_to_all | solution.py:57
  56.6 43.0 %all-to-all-start = ((bf16[32,1,48,1024]{3,2,1,0:T(8,128)(2,1)}), bf16[32,1,48,1024]{3,2,1,0:T(8,128)(2,1)}, u32[]{:S(2)}, u32[]{:S(2)}) async-start(bf16[32,1,48,1024]{3,2,1,0:T(8,128)(2,1)} %bitcast.46), calls=%async_computation | async-start | bytes 6291456 | tf_op jit(solution)/shard_map/all_to_all | solution.py:58
  62.1 3.3 %copy-start.6 = (bf16[4,1024,512]{2,1,0:T(8,128)(2,1)S(1)}, bf16[4,1024,512]{2,1,0:T(8,128)(2,1)}, u32[]{:S(2)}) copy-start(bf16[4,1024,512]{2,1,0:T(8,128)(2,1)} %param.15) | copy-start | bytes 12582916
  62.5 4.7 %copy-start.3 = (bf16[4,8,1,48,1024]{4,3,1,0,2:T(8,128)(2,1)}, bf16[4,8,1,48,1024]{4,3,1,0,2:T(8,128)(2,1)S(1)}, u32[]{:S(2)}) copy-start(bf16[4,8,1,48,1024]{4,3,1,0,2:T(8,128)(2,1)S(1)} %copy.33) | copy-start | bytes 9437188
  65.4 2.2 %copy-start.12 = (bf16[4,1024,512]{2,1,0:T(8,128)(2,1)S(1)}, bf16[4,1024,512]{2,1,0:T(8,128)(2,1)}, u32[]{:S(2)}) copy-start(bf16[4,1024,512]{2,1,0:T(8,128)(2,1)} %param.17) | copy-start | bytes 12582916
  67.6 41.2 %copy-start.14 = (bf16[4,384,512]{2,1,0:T(8,128)(2,1)}, bf16[4,384,512]{2,1,0:T(8,128)(2,1)S(1)}, u32[]{:S(2)}) copy-start(bf16[4,384,512]{2,1,0:T(8,128)(2,1)S(1)} %convolution_convert_fusion) | copy-start | bytes 4718596
  69.4 32.5 %copy-start.16 = (bf16[4,384,512]{2,1,0:T(8,128)(2,1)}, bf16[4,384,512]{2,1,0:T(8,128)(2,1)S(1)}, u32[]{:S(2)}) copy-start(bf16[4,384,512]{2,1,0:T(8,128)(2,1)S(1)} %convolution_convert_fusion.1) | copy-start | bytes 4718596
  99.5 3.1 %copy-start.11 = (bf16[4,512,1024]{2,1,0:T(8,128)(2,1)S(1)}, bf16[4,512,1024]{2,1,0:T(8,128)(2,1)}, u32[]{:S(2)}) copy-start(bf16[4,512,1024]{2,1,0:T(8,128)(2,1)} %param.16) | copy-start | bytes 12582916
  101.9 5.1 %copy-start.8 = (bf16[4,8,1,48,1024]{4,3,1,0,2:T(8,128)(2,1)}, bf16[4,8,1,48,1024]{4,3,1,0,2:T(8,128)(2,1)S(1)}, u32[]{:S(2)}) copy-start(bf16[4,8,1,48,1024]{4,3,1,0,2:T(8,128)(2,1)S(1)} %copy.31) | copy-start | bytes 9437188
  102.7 4.3 %copy-start.7 = (bf16[4,1024,512]{2,1,0:T(8,128)(2,1)S(1)}, bf16[4,1024,512]{2,1,0:T(8,128)(2,1)}, u32[]{:S(2)}) copy-start(bf16[4,1024,512]{2,1,0:T(8,128)(2,1)} %param.15) | copy-start | bytes 12582916
  107.0 1.8 %copy-start.5 = (bf16[4,384,512]{2,1,0:T(8,128)(2,1)}, bf16[4,384,512]{2,1,0:T(8,128)(2,1)S(1)}, u32[]{:S(2)}) copy-start(bf16[4,384,512]{2,1,0:T(8,128)(2,1)S(1)} %get-tuple-element.9) | copy-start | bytes 4718596
  107.0 2.8 %copy-start.13 = (bf16[4,1024,512]{2,1,0:T(8,128)(2,1)S(1)}, bf16[4,1024,512]{2,1,0:T(8,128)(2,1)}, u32[]{:S(2)}) copy-start(bf16[4,1024,512]{2,1,0:T(8,128)(2,1)} %param.17) | copy-start | bytes 12582916
  115.6 41.9 %all-to-all-start.2 = ((bf16[4,8,48,1024]{3,2,0,1:T(8,128)(2,1)}), bf16[4,8,48,1024]{3,2,0,1:T(8,128)(2,1)S(1)}, u32[]{:S(2)}, u32[]{:S(2)}) async-start(bf16[4,8,48,1024]{3,2,0,1:T(8,128)(2,1)} %copy.34), calls=%async_computation.2 | async-start | bytes 6291456 | tf_op jit(solution)/shard_map/all_to_all | solution.py:60
  120.6 8.3 %copy-start.9 = (bf16[4,8,1,48,1024]{4,3,1,0,2:T(8,128)(2,1)S(1)}, bf16[4,8,1,48,1024]{4,3,1,0,2:T(8,128)(2,1)}, u32[]{:S(2)}) copy-start(bf16[4,8,1,48,1024]{4,3,1,0,2:T(8,128)(2,1)} %copy-done.8) | copy-start | bytes 9437188
  120.6 8.3 %copy-start.15 = (bf16[4,384,512]{2,1,0:T(8,128)(2,1)S(1)}, bf16[4,384,512]{2,1,0:T(8,128)(2,1)}, u32[]{:S(2)}) copy-start(bf16[4,384,512]{2,1,0:T(8,128)(2,1)} %copy-done.14) | copy-start | bytes 4718596
  120.6 8.3 %copy-start.17 = (bf16[4,384,512]{2,1,0:T(8,128)(2,1)S(1)}, bf16[4,384,512]{2,1,0:T(8,128)(2,1)}, u32[]{:S(2)}) copy-start(bf16[4,384,512]{2,1,0:T(8,128)(2,1)} %copy-done.16) | copy-start | bytes 4718596
  128.9 6.0 %copy-start.4 = (bf16[4,8,1,48,1024]{4,3,1,0,2:T(8,128)(2,1)S(1)}, bf16[4,8,1,48,1024]{4,3,1,0,2:T(8,128)(2,1)}, u32[]{:S(2)}) copy-start(bf16[4,8,1,48,1024]{4,3,1,0,2:T(8,128)(2,1)} %copy-done.3) | copy-start | bytes 9437188
  128.9 6.0 %copy-start.18 = (f32[4,384,512]{2,1,0:T(8,128)S(1)}, f32[4,384,512]{2,1,0:T(8,128)}, u32[]{:S(2)}) copy-start(f32[4,384,512]{2,1,0:T(8,128)} %get-tuple-element.10) | copy-start | bytes 9437188
  157.6 8.7 %copy-start.1 = (bf16[128,1024]{1,0:T(8,128)(2,1)S(1)}, bf16[128,1024]{1,0:T(8,128)(2,1)}, u32[]{:S(2)}) copy-start(bf16[128,1024]{1,0:T(8,128)(2,1)} %param.10) | copy-start | bytes 786436
where the time goes:
time: 167 us; the launch traced here: 166 us
  waiting for transfers between devices  68.6 us (41%)
  local copies, waits for them, and re-layouts  36.8 us (22%)
  matrix products  33.7 us (20%)
  starting transfers between devices  16.3 us (10%)
  other arithmetic  10 us (6%)
    all_to_all x1, waiting for transfers between devices, local_step(): lax.all_to_all(dz_send.reshape(n_exp, 1, cap_rows, d_model), 'ep', 0, 1,...  30.1 us
    all_to_all x1, waiting for transfers between devices, local_step(): lax.all_to_all(x_send.reshape(n_exp, 1, cap_rows, d_model), 'ep', 0, 1, t...  21.7 us
    all_to_all x1, waiting for transfers between devices, local_step(): lax.all_to_all(dx_rows.reshape(n_local, n_dev, cap_rows, d_model), 'ep',...  16.8 us
    dot_general x1, matrix products, expert_backward(): jnp.einsum('erd,erf->edf', x_rows, d_gate, preferred_element_type=jnp.flo...  8.29 us
    all_to_all x1, starting transfers between devices, local_step(): lax.all_to_all(x_send.reshape(n_exp, 1, cap_rows, d_model), 'ep', 0, 1, t...  6.15 us
    dot_general x1, matrix products, expert_backward(): jnp.einsum('erf,erd->efd', hidden, dz_rows, preferred_element_type=jnp.fl...  5.96 us
    dot_general x1, matrix products, expert_backward(): jnp.einsum('erd,erf->edf', x_rows, d_up, preferred_element_type=jnp.float32)  5.88 us
    gather x1, local copies, waits for them, and re-layouts, source_dispatch(): jnp.take(gate_src.reshape(n_copy), slot_copy, mode='fill', fill_value=0)  5.85 us
  transfers between devices with their start and end apart: 3, of which 3 were waited for; matrix products, arithmetic and copies ran while one was open for 24% of the time, Pallas kernels for 0%

commit v1 on v0

v1 whole, which is shorter than its diff:
```python
import functools

import jax
import jax.numpy as jnp
from jax import lax
from jax.experimental import pallas as pl
from jax.experimental.pallas import tpu as pltpu
from jax.sharding import PartitionSpec as P

BF = jnp.bfloat16
F32 = jnp.float32
COLS = 256


def slot_capacity(tok_dev, top_k, n_exp):
    return ((3 * tok_dev * top_k) // (2 * n_exp) + 7) // 8 * 8


def dot(a, b, ca=1, cb=0):
    return lax.dot_general(a, b, (((ca,), (cb,)), ((), ())), preferred_element_type=F32)


PASSES = (((0, 0), (0, 1), (2, 0), (2, 1)), ((1, 0), (1, 1), (3, 0), (3, 1)))


def route_kernel(
    n_dev, cap, x_hbm, y_hbm, meta_hbm, w1_hbm, w2_hbm, w3_hbm,
    xr_out, zr_out, h_out, da_out, db_out, own_out, right_out, left_out,
    xb, yb, mb, w1, w2, w3, xr, zr, hb, dab, dbb, dxb, oh, part, ddr, hopr, osum,
    send_sem, recv_sem, load_sem, out_sem,
):
    n_chip = n_dev // 2
    me = lax.axis_index("ep")
    chip, core = me // 2, me % 2
    right = {"ep": ((chip + 1) % n_chip) * 2 + core}
    left = {"ep": ((chip + n_chip - 1) % n_chip) * 2 + core}
    mate = {"ep": chip * 2 + 1 - core}
    n_loc, d_model, d_ff = w1.shape
    tok = x_hbm.shape[0]
    half = tok // 2
    rows = 4 * cap
    halves = (pl.ds(0, half), pl.ds(half, half))

    loads = [
        pltpu.make_async_copy(x_hbm, xb.at[0, 0], load_sem.at[0]),
        pltpu.make_async_copy(y_hbm, yb.at[0, 0], load_sem.at[1]),
        pltpu.make_async_copy(meta_hbm, mb.at[0, 0], load_sem.at[2]),
        pltpu.make_async_copy(w1_hbm, w1, load_sem.at[3]),
        pltpu.make_async_copy(w3_hbm, w3, load_sem.at[4]),
        pltpu.make_async_copy(w2_hbm, w2, load_sem.at[5]),
    ]
    for c in loads:
        c.start()

    barrier = pltpu.get_barrier_semaphore()
    for peer in (right, left, mate):
        pl.semaphore_signal(barrier, inc=1, device_id=peer, device_id_type=pl.DeviceIdType.MESH)
    pl.semaphore_wait(barrier, 3)

    made = []

    def send(src, dst, peer):
        n = len(made)
        c = pltpu.make_async_remote_copy(
            src_ref=src, dst_ref=dst, send_sem=send_sem.at[n], recv_sem=recv_sem.at[n],
            device_id=peer, device_id_type=pl.DeviceIdType.MESH)
        c.start()
        made.append(c)
        return c

    for c in loads[:3]:
        c.wait()

    m_r = send(mb.at[0, 0], mb.at[3, 0], right)
    m_l = send(mb.at[0, 0], mb.at[1, 0], left)
    m_m = send(mb.at[0, 0], mb.at[0, 1], mate)
    x_r = [send(xb.at[0, 0, h], xb.at[3, 0, h], right) for h in halves]
    y_l = [send(yb.at[0, 0, h], yb.at[1, 0, h], left) for h in halves]
    x_m = send(xb.at[0, 0], xb.at[0, 1], mate)
    y_m = send(yb.at[0, 0], yb.at[0, 1], mate)

    m_r.wait_recv()
    m_f = send(mb.at[3, 0], mb.at[2, 0], right)
    m_r2 = send(mb.at[3, 0], mb.at[3, 1], mate)
    m_l.wait_recv()
    m_l2 = send(mb.at[1, 0], mb.at[1, 1], mate)
    x_f, y_f = [], []
    for i, h in enumerate(halves):
        x_r[i].wait_recv()
        x_f.append(send(xb.at[3, 0, h], xb.at[2, 0, h], right))
        y_l[i].wait_recv()
        y_f.append(send(yb.at[1, 0, h], yb.at[2, 0, h], left))
    y_r = send(yb.at[0, 0], yb.at[3, 0], right)
    x_l = send(xb.at[0, 0], xb.at[1, 0], left)
    m_f.wait_recv()
    m_f2 = send(mb.at[2, 0], mb.at[2, 1], mate)
    x_f2, y_f2 = [], []
    for i, h in enumerate(halves):
        x_f[i].wait_recv()
        x_f2.append(send(xb.at[2, 0, h], xb.at[2, 1, h], mate))
        y_f[i].wait_recv()
        y_f2.append(send(yb.at[2, 0, h], yb.at[2, 1, h], mate))
    x_m.wait_recv()
    y_m.wait_recv()
    m_m.wait_recv()

    for c in loads[3:]:
        c.wait()

    row_id = lax.broadcasted_iota(jnp.int32, (n_loc * cap, tok), 0) + me * (n_loc * cap)

    def place(p, i):
        d, k = PASSES[p][i]
        q = 4 * p + i
        keys = mb[d, k, 0:8, :].astype(jnp.int32)
        gates = mb[d, k, 8:16, :]
        hot = jnp.zeros((n_loc * cap, tok), F32)
        gate = jnp.zeros((n_loc * cap, tok), F32)
        for j in range(8):
            hit = keys[j:j + 1, :] == row_id
            hot = jnp.where(hit, 1.0, hot)
            gate = jnp.where(hit, gates[j:j + 1, :], gate)
        gate_row = jnp.sum(gate, axis=1, keepdims=True)
        hot = hot.astype(BF)
        oh[q] = hot
        for n in range(d_model // COLS):
            cols = pl.ds(n * COLS, COLS)
            xv = dot(hot, xb[d, k, :, cols]).astype(BF)
            zv = (dot(hot, yb[d, k, :, cols]) * gate_row).astype(BF)
            for e in range(n_loc):
                xr[e, pl.ds(q * cap, cap), cols] = xv[e * cap:(e + 1) * cap]
                zr[e, pl.ds(q * cap, cap), cols] = zv[e * cap:(e + 1) * cap]

    def experts(p):
        at = pl.ds(p * rows, rows)

        def one(e, carry):
            x_e = xr[e, at, :]
            z_e = zr[e, at, :]
            for n in range(d_ff // COLS):
                cols = pl.ds(n * COLS, COLS)
                a = dot(x_e, w1[e, :, cols]).astype(BF).astype(F32)
                b = dot(x_e, w3[e, :, cols]).astype(BF).astype(F32)
                dh = dot(z_e, w2[e, cols, :], 1, 1)
                sg = jax.nn.sigmoid(a)
                act = a * sg
                hb[e, at, cols] = (act * b).astype(BF)
                dab[e, at, cols] = (dh * b * sg * (1.0 + a * (1.0 - sg))).astype(BF)
                dbb[e, at, cols] = (dh * act).astype(BF)
            da = dab[e, at, :]
            db = dbb[e, at, :]
            for n in range(d_model // COLS):
                cols = pl.ds(n * COLS, COLS)
                dxb[e, :, cols] = (dot(da, w1[e, cols, :], 1, 1) + dot(db, w3[e, cols, :], 1, 1)).astype(BF)
            return carry

        lax.fori_loop(0, n_loc, one, 0)

    def combine(p, i):
        q = 4 * p + i
        for n in range(d_model // COLS):
            cols = pl.ds(n * COLS, COLS)
            back = jnp.concatenate([dxb[e, pl.ds(i * cap, cap), cols] for e in range(n_loc)], axis=0)
            part[q, :, cols] = dot(oh[q], back, 0, 0)

    def stash(p):
        at = pl.ds(p * rows, rows)
        out = []
        for t, (src, dst) in enumerate(((xr, xr_out), (zr, zr_out), (hb, h_out), (dab, da_out), (dbb, db_out))):
            c = pltpu.make_async_copy(src.at[:, at, :], dst.at[:, at, :], out_sem.at[5 * p + t])
            c.start()
            out.append(c)
        return out

    place(0, 0)
    place(0, 1)
    m_f2.wait_recv()
    for i in range(2):
        x_f2[i].wait_recv()
        y_f2[i].wait_recv()
    place(0, 2)
    place(0, 3)
    experts(0)
    outs = stash(0)

    y_r.wait_recv()
    y_r2 = send(yb.at[3, 0], yb.at[3, 1], mate)
    x_l.wait_recv()
    x_l2 = send(xb.at[1, 0], xb.at[1, 1], mate)
    x_r2 = send(xb.at[3, 0], xb.at[3, 1], mate)
    y_l2 = send(yb.at[1, 0], yb.at[1, 1], mate)

    combine(0, 3)
    d_opp = send(part.at[3], ddr.at[1], mate)
    combine(0, 2)
    combine(0, 1)
    d_own = send(part.at[1], ddr.at[0], mate)
    combine(0, 0)
    d_opp.wait_recv()
    osum[...] = part[2] + ddr[1]
    hop_r = send(osum.at[pl.ds(0, half)], hopr.at[0], right)
    hop_l = send(osum.at[pl.ds(half, half)], hopr.at[1], left)

    m_r2.wait_recv()
    m_l2.wait_recv()
    place(1, 0)
    place(1, 2)
    y_r2.wait_recv()
    x_l2.wait_recv()
    x_r2.wait_recv()
    y_l2.wait_recv()
    place(1, 1)
    place(1, 3)
    experts(1)
    outs += stash(1)
    combine(1, 1)
    d_right = send(part.at[5], ddr.at[2], mate)
    combine(1, 3)
    d_left = send(part.at[7], ddr.at[3], mate)
    combine(1, 0)
    combine(1, 2)
    d_own.wait_recv()
    part[0] += ddr[0]
    d_right.wait_recv()
    d_left.wait_recv()
    hop_r.wait_recv()
    hop_l.wait_recv()
    part[4] += ddr[2]
    part[6] += ddr[3]
    part[4, pl.ds(0, half)] += hopr[0]
    part[6, pl.ds(half, half)] += hopr[1]
    for t, (q, dst) in enumerate(((0, own_out), (4, right_out), (6, left_out))):
        c = pltpu.make_async_copy(part.at[q], dst, out_sem.at[10 + t])
        c.start()
        outs.append(c)
    for c in outs:
        c.wait()
    for c in made:
        c.wait_send()


def route(n_dev, cap, x, y, meta, w1, w2, w3):
    n_loc, d_model, d_ff = w1.shape
    tok = x.shape[0]
    n_rows = n_dev * cap
    any_spec = pl.BlockSpec(memory_space=pl.ANY)
    flops = 2 * n_loc * n_rows * d_model * d_ff * 5
    return pl.pallas_call(
        functools.partial(route_kernel, n_dev, cap),
        out_shape=(
            jax.ShapeDtypeStruct((n_loc, n_rows, d_model), BF),
            jax.ShapeDtypeStruct((n_loc, n_rows, d_model), BF),
            jax.ShapeDtypeStruct((n_loc, n_rows, d_ff), BF),
            jax.ShapeDtypeStruct((n_loc, n_rows, d_ff), BF),
            jax.ShapeDtypeStruct((n_loc, n_rows, d_ff), BF),
            jax.ShapeDtypeStruct((tok, d_model), F32),
            jax.ShapeDtypeStruct((tok, d_model), F32),
            jax.ShapeDtypeStruct((tok, d_model), F32),
        ),
        in_specs=[any_spec] * 6,
        out_specs=[any_spec] * 8,
        scratch_shapes=[
            pltpu.VMEM((4, 2, tok, d_model), BF),
            pltpu.VMEM((4, 2, tok, d_model), BF),
            pltpu.VMEM((4, 2, 16, tok), F32),
            pltpu.VMEM(w1.shape, BF),
            pltpu.VMEM(w2.shape, BF),
            pltpu.VMEM(w3.shape, BF),
            pltpu.VMEM((n_loc, n_rows, d_model), BF),
            pltpu.VMEM((n_loc, n_rows, d_model), BF),
            pltpu.VMEM((n_loc, n_rows, d_ff), BF),
            pltpu.VMEM((n_loc, n_rows, d_ff), BF),
            pltpu.VMEM((n_loc, n_rows, d_ff), BF),
            pltpu.VMEM((n_loc, 4 * cap, d_model), BF),
            pltpu.VMEM((8, n_loc * cap, tok), BF),
            pltpu.VMEM((8, tok, d_model), F32),
            pltpu.VMEM((4, tok, d_model), F32),
            pltpu.VMEM((2, tok // 2, d_model), F32),
            pltpu.VMEM((tok, d_model), F32),
            pltpu.SemaphoreType.DMA((40,)),
            pltpu.SemaphoreType.DMA((40,)),
            pltpu.SemaphoreType.DMA((6,)),
            pltpu.SemaphoreType.DMA((13,)),
        ],
        compiler_params=pltpu.CompilerParams(
            collective_id=0, has_side_effects=True, vmem_limit_bytes=56 * 1024 * 1024),
        cost_estimate=pl.CostEstimate(flops=flops, bytes_accessed=24 * 1024 * 1024, transcendentals=0),
        name="route",
    )(x, y, meta, w1, w2, w3)


def grad_kernel(x_ref, z_ref, h_ref, da_ref, db_ref, g1_ref, g2_ref, g3_ref):
    x = x_ref[0]
    g1_ref[0] = dot(x, da_ref[0], 0, 0)
    g3_ref[0] = dot(x, db_ref[0], 0, 0)
    g2_ref[0] = dot(h_ref[0], z_ref[0], 0, 0)


def grads(xr, zr, h, da, db, parts=2):
    n_loc, n_rows, d_model = xr.shape
    d_ff = h.shape[2]
    bm, bf = d_model // parts, d_ff // parts
    full = lambda width: pl.BlockSpec((1, n_rows, width), lambda e, i: (e, 0, 0))
    part = lambda width: pl.BlockSpec((1, n_rows, width), lambda e, i: (e, 0, i))
    return pl.pallas_call(
        grad_kernel,
        grid=(n_loc, parts),
        in_specs=[part(bm), full(d_model), part(bf), full(d_ff), full(d_ff)],
        out_specs=[
            pl.BlockSpec((1, bm, d_ff), lambda e, i: (e, i, 0)),
            pl.BlockSpec((1, bf, d_model), lambda e, i: (e, i, 0)),
            pl.BlockSpec((1, bm, d_ff), lambda e, i: (e, i, 0)),
        ],
        out_shape=(
            jax.ShapeDtypeStruct((n_loc, d_model, d_ff), F32),
            jax.ShapeDtypeStruct((n_loc, d_ff, d_model), F32),
            jax.ShapeDtypeStruct((n_loc, d_model, d_ff), F32),
        ),
        compiler_params=pltpu.CompilerParams(
            dimension_semantics=("arbitrary", "arbitrary"), vmem_limit_bytes=60 * 1024 * 1024),
        cost_estimate=pl.CostEstimate(
            flops=6 * n_loc * n_rows * d_model * d_ff, bytes_accessed=36 * 1024 * 1024, transcendentals=0),
        name="grads",
    )(xr, zr, h, da, db)


def solution(mesh):
    n_dev = mesh.shape["ep"]
    n_chip = n_dev // 2
    to_right = [(i, ((i // 2 + 1) % n_chip) * 2 + i % 2) for i in range(n_dev)]
    to_left = [(j, i) for i, j in to_right]

    def local_step(x_loc, dy_loc, ids_loc, gate_loc, slot_loc, w_gate, w_down, w_up):
        tok_dev, top_k = ids_loc.shape
        n_exp = w_gate.shape[0] * n_dev
        cap = slot_capacity(tok_dev, top_k, n_exp)
        key = jnp.where(slot_loc >= 0, ids_loc * cap + slot_loc, -1)
        meta = jnp.concatenate([key.astype(F32).T, gate_loc.T], axis=0)
        xr, zr, h, da, db, own, right, left = route(n_dev, cap, x_loc, dy_loc, meta, w_gate, w_down, w_up)
        from_left = lax.ppermute(right, "ep", to_right)
        from_right = lax.ppermute(left, "ep", to_left)
        g_gate, g_down, g_up = grads(xr, zr, h, da, db)
        dx = (own + from_left + from_right).astype(BF)
        return dx, g_gate, g_down, g_up

    tok_spec = P(("dp", "ep"), None)
    w_spec = P("ep", None, None)
    grad_spec = P(("dp", "ep"), None, None)
    return jax.shard_map(
        local_step, mesh=mesh,
        in_specs=(tok_spec, tok_spec, tok_spec, tok_spec, tok_spec, w_spec, w_spec, w_spec),
        out_specs=(tok_spec, grad_spec, grad_spec, grad_spec), check_vma=False)
```

time: 167 us -> 66.6 us (0.40)
  waiting for transfers between devices: 68.6 us -> 0.01 us
  Pallas kernels: 0 us -> 60.1 us
  local copies, waits for them, and re-layouts: 36.8 us -> 0.01 us
  matrix products: 33.7 us -> 0 us
  starting transfers between devices: 16.3 us -> 2.76 us
  other arithmetic: 10 us -> 2.79 us
    all_to_all x3 -> x0, waiting for transfers between devices: 68.6 us -> none  [the longest x1 30.1 us: local_step(): lax.all_to_all(dz_send.reshape(n_exp, 1, cap_rows, d_model), 'ep', 0, 1,...]
    pallas_call x0 -> x2, Pallas kernels: none -> 60.1 us  [the longest x1 42.6 us: route(): pl.pallas_call(functools.partial(route_kernel, n_dev, cap), out_shape=(ja...]
    dot_general x8 -> x0, matrix products: 33.7 us -> none  [the longest x1 8.29 us: expert_backward(): jnp.einsum('erd,erf->edf', x_rows, d_gate, preferred_element_type=jnp.flo...]
    gather x4 -> x0, local copies, waits for them, and re-layouts: 22 us -> none  [the longest x1 5.85 us: source_dispatch(): jnp.take(gate_src.reshape(n_copy), slot_copy, mode='fill', fill_value=0)]
    all_to_all x3 -> x0, starting transfers between devices: 16.3 us -> none  [the longest x1 6.15 us: local_step(): lax.all_to_all(x_send.reshape(n_exp, 1, cap_rows, d_model), 'ep', 0, 1, t...]
    unnamed x39 -> x2, local copies, waits for them, and re-layouts: 5.1 us -> 0.01 us
    scatter x1 -> x0, local copies, waits for them, and re-layouts: 4.32 us -> none  [source_dispatch(): jnp.full((n_exp * cap_rows,), n_copy, jnp.int32)]
    reduce_sum x1 -> x0, other arithmetic: 3.41 us -> none  [source_combine(): return jnp.sum(rows, axis=1, dtype=jnp.float32).astype(jnp.bfloat16)]
  transfers between devices with their start and end apart: 3 -> 2, of which waited for: 3 -> 0; matrix products, arithmetic and copies ran while one was open for 24% -> 0% of each run, Pallas kernels for 0% -> 26%
where the time goes in v1:
time: 66.6 us; the launch traced here: 66.3 us
  Pallas kernels  60.1 us (90%)
  other arithmetic  2.79 us (4%)
  starting transfers between devices  2.76 us (4%)
    pallas_call x1, Pallas kernels, route(): pl.pallas_call(functools.partial(route_kernel, n_dev, cap), out_shape=(ja...  42.6 us
    pallas_call x1, Pallas kernels, grads(): pl.pallas_call(grad_kernel, grid=(n_loc, parts), in_specs=[part(bm), full...  17.5 us
    ppermute x1, starting transfers between devices, local_step(): from_right = lax.ppermute(left, 'ep', to_left)  1.95 us
  transfers between devices with their start and end apart: 2, of which 0 were waited for; matrix products, arithmetic and copies ran while one was open for 0% of the time, Pallas kernels for 26%

profile of v1, /device:TPU:81, one launch (start us, length us, event | category | flops | bytes accessed | tf_op | source)
XLA Modules:
  0.0 66.3 jit_solution(2111002186821679855)
XLA Ops:
  0.6 0.7 %convert_bitcast_fusion = f32[8,128]{1,0:T(8,128)S(1)} fusion(s32[128,8]{0,1:T(8,128)} %param.12, s32[128,8]{0,1:T(8,128)} %param.10), kind=kLoop, calls=%fused_computation.2 | loop fusion | flops 5120 | bytes 12288 | tf_op jit(solution)/shard_map/transpose | solution.py:338
  1.3 1.3 %pad_maximum_fusion.meta_hbm = f32[16,128]{1,0:T(8,128)} fusion(f32[8,128]{1,0:T(8,128)} %bitcast.3, f32[8,128]{1,0:T(8,128)S(1)} %convert_bitcast_fusion), kind=kLoop, calls=%fused_computation.1 | loop fusion | flops 2048 | bytes 16384 | tf_op jit(solution)/shard_map/concatenate | solution.py:338
  2.6 42.6 %route.1 = (bf16[4,384,1024]{2,1,0:T(8,128)(2,1)}, bf16[4,384,1024]{2,1,0:T(8,128)(2,1)}, bf16[4,384,512]{2,1,0:T(8,128)(2,1)}, bf16[4,384,512]{2,1,0:T(8,128)(2...) custom-call(bf16[128,1024]{1,0:T(8,128)(2,1)} %x_hbm.1, ...), custom_call_target="tpu_custom_call" | custom-call | flops 8053063680 | bytes 25165824 | tf_op jit(solution)/shard_map/route/pallas_call | solution.py:248
  45.2 0.8 %collective-permute-start = (f32[128,1024]{1,0:T(8,128)}, f32[128,1024]{1,0:T(8,128)S(1)}, u32[]{:S(2)}, u32[]{:S(2)}) collective-permute-start(f32[128,1024]{1,0:T(8,128)} %get-tuple-element.16), channel_id=1, source_target_pairs={{0,2},{1,3},{2,4},{3,5},{4,6},{5,7},{6,0},{7,1},{8,10},{9,11},{10,... | collective-permute-start | bytes 1572872 | tf_op jit(solution)/shard_map/ppermute | solution.py:340
  46.0 2.0 %collective-permute-start.1 = (f32[128,1024]{1,0:T(8,128)}, f32[128,1024]{1,0:T(8,128)S(1)}, u32[]{:S(2)}, u32[]{:S(2)}) collective-permute-start(f32[128,1024]{1,0:T(8,128)} %get-tuple-element.17), channel_id=1, source_target_pairs={{2,0},{3,1},{4,2},{5,3},{6,4},{7,5},{0,6},{1,7},{10,8},{11,9},{12,... | collective-permute-start | bytes 1572872 | tf_op jit(solution)/shard_map/ppermute | solution.py:341
  48.0 0.0 copy-start
  48.0 17.5 %grads.1 = (f32[4,1024,512]{2,1,0:T(8,128)}, f32[4,512,1024]{2,1,0:T(8,128)}, f32[4,1024,512]{2,1,0:T(8,128)}) custom-call(bf16[4,384,1024]{2,1,0:T(8,128)(2,1)} %get-tuple-element.18.x_ref, bf16[4,384,1024]{2,1,0:T(8,128)(2,1)} %get-tuple-element.19.z_ref, bf16[4,384,512]{2,1,0:T(8,128)(2,1)} %get-tuple-element.20.h_ref, ...), custom_call_target="tpu_custom_call" | custom-call | flops 4831838208 | bytes 37748736 | tf_op jit(solution)/shard_map/grads/pallas_call | solution.py:305
  65.5 0.0 collective-permute-done
  65.5 0.0 collective-permute-done.1
  65.5 0.0 copy-done
  65.5 0.8 %add_convert_fusion = bf16[128,1024]{1,0:T(8,128)(2,1)} fusion(f32[128,1024]{1,0:T(8,128)S(1)} %collective-permute-done.1, f32[128,1024]{1,0:T(8,128)S(1)} %copy-done, f32[128,1024]{1,0:T(8,128)S(1)} %collective-permute-done), kind=kLoop, calls=%fused_computation | loop fusion | flops 393216 | bytes 1835008 | tf_op jit(solution)/shard_map/convert_element_type | solution.py:343
Async XLA Ops:
  45.2 20.2 %collective-permute-start = (f32[128,1024]{1,0:T(8,128)}, f32[128,1024]{1,0:T(8,128)S(1)}, u32[]{:S(2)}, u32[]{:S(2)}) collective-permute-start(f32[128,1024]{1,0:T(8,128)} %get-tuple-element.16), channel_id=1, source_target_pairs={{0,2},{1,3},{2,4},{3,5},{4,6},{5,7},{6,0},{7,1},{8,10},{9,11},{10,... | collective-permute-start | bytes 1572872 | tf_op jit(solution)/shard_map/ppermute | solution.py:340
  46.0 19.4 %collective-permute-start.1 = (f32[128,1024]{1,0:T(8,128)}, f32[128,1024]{1,0:T(8,128)S(1)}, u32[]{:S(2)}, u32[]{:S(2)}) collective-permute-start(f32[128,1024]{1,0:T(8,128)} %get-tuple-element.17), channel_id=1, source_target_pairs={{2,0},{3,1},{4,2},{5,3},{6,4},{7,5},{0,6},{1,7},{10,8},{11,9},{12,... | collective-permute-start | bytes 1572872 | tf_op jit(solution)/shard_map/ppermute | solution.py:341
  48.0 17.5 %copy-start = (f32[128,1024]{1,0:T(8,128)S(1)}, f32[128,1024]{1,0:T(8,128)}, u32[]{:S(2)}) copy-start(f32[128,1024]{1,0:T(8,128)} %get-tuple-element.15) | copy-start | bytes 1572868

commit v2 on v1

v2 whole, which is shorter than its diff:
```python
import functools

import jax
import jax.numpy as jnp
from jax import lax
from jax.experimental import pallas as pl
from jax.experimental.pallas import tpu as pltpu
from jax.sharding import PartitionSpec as P

BF = jnp.bfloat16
F32 = jnp.float32
COLS = 256


def slot_capacity(tok_dev, top_k, n_exp):
    return ((3 * tok_dev * top_k) // (2 * n_exp) + 7) // 8 * 8


def dot(a, b, ca=1, cb=0):
    return lax.dot_general(a, b, (((ca,), (cb,)), ((), ())), preferred_element_type=F32)


PASSES = (((0, 0), (0, 1)), ((2, 0), (2, 1)), ((1, 0), (1, 1), (3, 0), (3, 1)))
FIRST = (0, 2, 4)


def route_kernel(
    n_dev, cap, x_hbm, y_hbm, ids_hbm, slots_hbm, gates_hbm, w1_hbm, w2_hbm, w3_hbm,
    xr, zr, hb, dab, dbb, own_out, right_out, left_out,
    xb, yb, mb, w1, w2, w3, dxb, oh, part, ddr, hopr, osum, ids, slots, gates,
    send_sem, recv_sem, load_sem,
):
    n_chip = n_dev // 2
    me = lax.axis_index("ep")
    chip, core = me // 2, me % 2
    right = {"ep": ((chip + 1) % n_chip) * 2 + core}
    left = {"ep": ((chip + n_chip - 1) % n_chip) * 2 + core}
    mate = {"ep": chip * 2 + 1 - core}
    n_loc, d_model, d_ff = w1.shape
    top_k, tok = ids.shape
    half = tok // 2
    halves = (pl.ds(0, half), pl.ds(half, half))

    loads = [
        pltpu.make_async_copy(src, dst, load_sem.at[i])
        for i, (src, dst) in enumerate((
            (x_hbm, xb.at[0, 0]), (y_hbm, yb.at[0, 0]), (ids_hbm, ids), (slots_hbm, slots), (gates_hbm, gates),
            (w1_hbm, w1), (w3_hbm, w3), (w2_hbm, w2)))
    ]
    for c in loads[:5]:
        c.start()

    barrier = pltpu.get_barrier_semaphore()
    for peer in (right, left, mate):
        pl.semaphore_signal(barrier, inc=1, device_id=peer, device_id_type=pl.DeviceIdType.MESH)

    for c in loads[2:5]:
        c.wait()
    mb[0, 0, 0:top_k, :] = jnp.where(slots[...] >= 0, ids[...] * cap + slots[...], -1).astype(F32)
    mb[0, 0, top_k:2 * top_k, :] = gates[...]

    for c in loads[:2]:
        c.wait()
    pl.semaphore_wait(barrier, 3)

    made = []

    def send(src, dst, peer):
        n = len(made)
        c = pltpu.make_async_remote_copy(
            src_ref=src, dst_ref=dst, send_sem=send_sem.at[n], recv_sem=recv_sem.at[n],
            device_id=peer, device_id_type=pl.DeviceIdType.MESH)
        c.start()
        made.append(c)
        return c

    x_r, y_l = [], []
    for h in halves:
        x_r.append(send(xb.at[0, 0, h], xb.at[3, 0, h], right))
        y_l.append(send(yb.at[0, 0, h], yb.at[1, 0, h], left))
    x_m = send(xb.at[0, 0], xb.at[0, 1], mate)
    m_m = send(mb.at[0, 0], mb.at[0, 1], mate)
    y_m = send(yb.at[0, 0], yb.at[0, 1], mate)
    m_r = send(mb.at[0, 0], mb.at[3, 0], right)
    m_l = send(mb.at[0, 0], mb.at[1, 0], left)
    for c in loads[5:]:
        c.start()

    row_id = lax.broadcasted_iota(jnp.int32, (n_loc * cap, tok), 0) + me * (n_loc * cap)

    def place(p, i):
        d, k = PASSES[p][i]
        q = FIRST[p] + i
        keys = mb[d, k, 0:top_k, :].astype(jnp.int32)
        gate_of = mb[d, k, top_k:2 * top_k, :]
        hot = jnp.zeros((n_loc * cap, tok), F32)
        gate = jnp.zeros((n_loc * cap, tok), F32)
        for j in range(top_k):
            hit = keys[j:j + 1, :] == row_id
            hot = jnp.where(hit, 1.0, hot)
            gate = jnp.where(hit, gate_of[j:j + 1, :], gate)
        gate_row = jnp.sum(gate, axis=1, keepdims=True)
        hot = hot.astype(BF)
        oh[q] = hot
        for n in range(d_model // COLS):
            cols = pl.ds(n * COLS, COLS)
            xv = dot(hot, xb[d, k, :, cols]).astype(BF)
            zv = (dot(hot, yb[d, k, :, cols]) * gate_row).astype(BF)
            for e in range(n_loc):
                xr[e, pl.ds(q * cap, cap), cols] = xv[e * cap:(e + 1) * cap]
                zr[e, pl.ds(q * cap, cap), cols] = zv[e * cap:(e + 1) * cap]

    def experts(p, lo, hi):
        rows = len(PASSES[p]) * cap
        at = pl.ds(FIRST[p] * cap, rows)

        def one(e, carry):
            x_e = xr[e, at, :]
            z_e = zr[e, at, :]
            for n in range(d_ff // COLS):
                cols = pl.ds(n * COLS, COLS)
                a = dot(x_e, w1[e, :, cols]).astype(BF).astype(F32)
                b = dot(x_e, w3[e, :, cols]).astype(BF).astype(F32)
                dh = dot(z_e, w2[e, cols, :], 1, 1)
                sg = jax.nn.sigmoid(a)
                act = a * sg
                hb[e, at, cols] = (act * b).astype(BF)
                dab[e, at, cols] = (dh * b * sg * (1.0 + a * (1.0 - sg))).astype(BF)
                dbb[e, at, cols] = (dh * act).astype(BF)
            da = dab[e, at, :]
            db = dbb[e, at, :]
            for n in range(d_model // COLS):
                cols = pl.ds(n * COLS, COLS)
                dxb[e, pl.ds(0, rows), cols] = (
                    dot(da, w1[e, cols, :], 1, 1) + dot(db, w3[e, cols, :], 1, 1)).astype(BF)
            return carry

        lax.fori_loop(lo, hi, one, 0)

    def combine(p, i):
        q = FIRST[p] + i
        for n in range(d_model // COLS):
            cols = pl.ds(n * COLS, COLS)
            back = jnp.concatenate([dxb[e, pl.ds(i * cap, cap), cols] for e in range(n_loc)], axis=0)
            part[q, :, cols] = dot(oh[q], back, 0, 0)

    def forward(i):
        x_r[i].wait_recv()
        x_f.append(send(xb.at[3, 0, halves[i]], xb.at[2, 0, halves[i]], right))
        y_l[i].wait_recv()
        y_f.append(send(yb.at[1, 0, halves[i]], yb.at[2, 0, halves[i]], left))

    x_f, y_f = [], []
    mid = n_loc // 2
    place(0, 0)
    for c in loads[5:]:
        c.wait()
    m_m.wait_recv()
    x_m.wait_recv()
    y_m.wait_recv()
    place(0, 1)
    experts(0, 0, mid)
    forward(0)
    experts(0, mid, n_loc)
    forward(1)
    m_r.wait_recv()
    m_f = send(mb.at[3, 0], mb.at[2, 0], right)
    y_r = send(yb.at[0, 0], yb.at[3, 0], right)
    x_l = send(xb.at[0, 0], xb.at[1, 0], left)
    m_l.wait_recv()
    early = [
        send(mb.at[3, 0], mb.at[3, 1], mate),
        send(mb.at[1, 0], mb.at[1, 1], mate),
        send(xb.at[3, 0], xb.at[3, 1], mate),
        send(yb.at[1, 0], yb.at[1, 1], mate),
    ]
    combine(0, 1)
    d_own = send(part.at[1], ddr.at[0], mate)
    combine(0, 0)

    opp = []
    for i, h in enumerate(halves):
        x_f[i].wait_recv()
        opp.append(send(xb.at[2, 0, h], xb.at[2, 1, h], mate))
        y_f[i].wait_recv()
        opp.append(send(yb.at[2, 0, h], yb.at[2, 1, h], mate))
    m_f.wait_recv()
    opp.append(send(mb.at[2, 0], mb.at[2, 1], mate))
    place(1, 0)
    for c in opp:
        c.wait_recv()
    place(1, 1)
    experts(1, 0, n_loc - 1)
    y_r.wait_recv()
    y_r2 = send(yb.at[3, 0], yb.at[3, 1], mate)
    x_l.wait_recv()
    x_l2 = send(xb.at[1, 0], xb.at[1, 1], mate)
    experts(1, n_loc - 1, n_loc)
    combine(1, 1)
    d_opp = send(part.at[3], ddr.at[1], mate)
    combine(1, 0)
    place(2, 0)
    place(2, 2)
    d_opp.wait_recv()
    osum[...] = part[2] + ddr[1]
    hop_r = send(osum.at[pl.ds(0, half)], hopr.at[0], right)
    hop_l = send(osum.at[pl.ds(half, half)], hopr.at[1], left)
    for c in early:
        c.wait_recv()
    y_r2.wait_recv()
    x_l2.wait_recv()
    place(2, 1)
    place(2, 3)
    experts(2, 0, n_loc)
    combine(2, 1)
    d_right = send(part.at[5], ddr.at[2], mate)
    combine(2, 3)
    d_left = send(part.at[7], ddr.at[3], mate)
    combine(2, 0)
    combine(2, 2)
    d_own.wait_recv()
    own_out[...] = part[0] + ddr[0]
    hop_r.wait_recv()
    hop_l.wait_recv()
    part[4, pl.ds(0, half)] += hopr[0]
    part[6, pl.ds(half, half)] += hopr[1]
    d_right.wait_recv()
    right_out[...] = part[4] + ddr[2]
    d_left.wait_recv()
    left_out[...] = part[6] + ddr[3]
    for c in made:
        c.wait_send()


def route(n_dev, cap, x, y, ids, slots, gates, w1, w2, w3):
    n_loc, d_model, d_ff = w1.shape
    top_k, tok = ids.shape
    n_rows = n_dev * cap
    hbm = pl.BlockSpec(memory_space=pltpu.HBM)
    vmem = pl.BlockSpec(memory_space=pltpu.VMEM)
    flops = 2 * n_loc * n_rows * d_model * d_ff * 5
    return pl.pallas_call(
        functools.partial(route_kernel, n_dev, cap),
        out_shape=(
            jax.ShapeDtypeStruct((n_loc, n_rows, d_model), BF),
            jax.ShapeDtypeStruct((n_loc, n_rows, d_model), BF),
            jax.ShapeDtypeStruct((n_loc, n_rows, d_ff), BF),
            jax.ShapeDtypeStruct((n_loc, n_rows, d_ff), BF),
            jax.ShapeDtypeStruct((n_loc, n_rows, d_ff), BF),
            jax.ShapeDtypeStruct((tok, d_model), F32),
            jax.ShapeDtypeStruct((tok, d_model), F32),
            jax.ShapeDtypeStruct((tok, d_model), F32),
        ),
        in_specs=[hbm] * 8,
        out_specs=[vmem] * 8,
        scratch_shapes=[
            pltpu.VMEM((4, 2, tok, d_model), BF),
            pltpu.VMEM((4, 2, tok, d_model), BF),
            pltpu.VMEM((4, 2, 2 * top_k, tok), F32),
            pltpu.VMEM(w1.shape, BF),
            pltpu.VMEM(w2.shape, BF),
            pltpu.VMEM(w3.shape, BF),
            pltpu.VMEM((n_loc, 4 * cap, d_model), BF),
            pltpu.VMEM((8, n_loc * cap, tok), BF),
            pltpu.VMEM((8, tok, d_model), F32),
            pltpu.VMEM((4, tok, d_model), F32),
            pltpu.VMEM((2, tok // 2, d_model), F32),
            pltpu.VMEM((tok, d_model), F32),
            pltpu.VMEM((top_k, tok), jnp.int32),
            pltpu.VMEM((top_k, tok), jnp.int32),
            pltpu.VMEM((top_k, tok), F32),
            pltpu.SemaphoreType.DMA((40,)),
            pltpu.SemaphoreType.DMA((40,)),
            pltpu.SemaphoreType.DMA((8,)),
        ],
        compiler_params=pltpu.CompilerParams(
            collective_id=0, has_side_effects=True, vmem_limit_bytes=36 * 1024 * 1024),
        cost_estimate=pl.CostEstimate(flops=flops, bytes_accessed=14 * 1024 * 1024, transcendentals=0),
        name="route",
    )(*(pltpu.with_memory_space_constraint(v, pltpu.HBM) for v in (x, y, ids, slots, gates, w1, w2, w3)))


def grad_kernel(x_ref, z_ref, h_ref, da_ref, db_ref, g1_ref, g2_ref, g3_ref):
    x = x_ref[0]
    g1_ref[0] = dot(x, da_ref[0], 0, 0)
    g3_ref[0] = dot(x, db_ref[0], 0, 0)
    g2_ref[0] = dot(h_ref[0], z_ref[0], 0, 0)


def grads(xr, zr, h, da, db, parts=2):
    n_loc, n_rows, d_model = xr.shape
    d_ff = h.shape[2]
    bm, bf = d_model // parts, d_ff // parts
    full = lambda width: pl.BlockSpec((1, n_rows, width), lambda e, i: (e, 0, 0))
    part = lambda width: pl.BlockSpec((1, n_rows, width), lambda e, i: (e, 0, i))
    return pl.pallas_call(
        grad_kernel,
        grid=(n_loc, parts),
        in_specs=[part(bm), full(d_model), part(bf), full(d_ff), full(d_ff)],
        out_specs=[
            pl.BlockSpec((1, bm, d_ff), lambda e, i: (e, i, 0)),
            pl.BlockSpec((1, bf, d_model), lambda e, i: (e, i, 0)),
            pl.BlockSpec((1, bm, d_ff), lambda e, i: (e, i, 0)),
        ],
        out_shape=(
            jax.ShapeDtypeStruct((n_loc, d_model, d_ff), F32),
            jax.ShapeDtypeStruct((n_loc, d_ff, d_model), F32),
            jax.ShapeDtypeStruct((n_loc, d_model, d_ff), F32),
        ),
        compiler_params=pltpu.CompilerParams(
            dimension_semantics=("arbitrary", "arbitrary"), vmem_limit_bytes=20 * 1024 * 1024),
        cost_estimate=pl.CostEstimate(
            flops=6 * n_loc * n_rows * d_model * d_ff, bytes_accessed=26 * 1024 * 1024, transcendentals=0),
        name="grads",
    )(xr, zr, h, da, db)


def solution(mesh):
    n_dev = mesh.shape["ep"]
    n_chip = n_dev // 2
    to_right = [(i, ((i // 2 + 1) % n_chip) * 2 + i % 2) for i in range(n_dev)]
    to_left = [(j, i) for i, j in to_right]

    def local_step(x_loc, dy_loc, ids_loc, gate_loc, slot_loc, w_gate, w_down, w_up):
        tok_dev, top_k = ids_loc.shape
        n_exp = w_gate.shape[0] * n_dev
        cap = slot_capacity(tok_dev, top_k, n_exp)
        xr, zr, h, da, db, own, right, left = route(
            n_dev, cap, x_loc, dy_loc, ids_loc.T, slot_loc.T, gate_loc.T, w_gate, w_down, w_up)
        from_left = lax.ppermute(right, "ep", to_right)
        from_right = lax.ppermute(left, "ep", to_left)
        g_gate, g_down, g_up = grads(xr, zr, h, da, db)
        dx = (own + from_left + from_right).astype(BF)
        return dx, g_gate, g_down, g_up

    tok_spec = P(("dp", "ep"), None)
    w_spec = P("ep", None, None)
    grad_spec = P(("dp", "ep"), None, None)
    return jax.shard_map(
        local_step, mesh=mesh,
        in_specs=(tok_spec, tok_spec, tok_spec, tok_spec, tok_spec, w_spec, w_spec, w_spec),
        out_specs=(tok_spec, grad_spec, grad_spec, grad_spec), check_vma=False)
```

time: 66.6 us -> 56.8 us (0.85)
  Pallas kernels: 60.1 us -> 51 us
  other arithmetic: 2.79 us -> 0.8 us
  waiting for transfers between devices: 0.01 us -> 1.51 us
    pallas_call x1, Pallas kernels: 17.5 us -> 10.5 us  [grads(): pl.pallas_call(grad_kernel, grid=(n_loc, parts), in_specs=[part(bm), full...]
    pallas_call x1, Pallas kernels: 42.6 us -> 40.5 us  [route(): pl.pallas_call(functools.partial(route_kernel, n_dev, cap), out_shape=(ja...]
    ppermute x1, waiting for transfers between devices: 0.01 us -> 1.51 us  [local_step(): from_left = lax.ppermute(right, 'ep', to_right)]
    concatenate x1 -> x0, other arithmetic: 1.29 us -> none  [local_step(): meta = jnp.concatenate([key.astype(F32).T, gate_loc.T], axis=0)]
    transpose x1 -> x0, other arithmetic: 0.71 us -> none  [local_step(): meta = jnp.concatenate([key.astype(F32).T, gate_loc.T], axis=0)]
  transfers between devices with their start and end apart: 2 -> 2, of which waited for: 0 -> 1; matrix products, arithmetic and copies ran while one was open for 0% -> 0% of each run, Pallas kernels for 26% -> 18%
where the time goes in v2:
time: 56.8 us; the launch traced here: 56.7 us
  Pallas kernels  51 us (90%)
  starting transfers between devices  2.76 us (5%)
  waiting for transfers between devices  1.51 us (3%)
  other arithmetic  0.8 us (1%)
  between operations  0.64 us (1%)
    pallas_call x1, Pallas kernels, route(): pl.pallas_call(functools.partial(route_kernel, n_dev, cap), out_shape=(ja...  40.5 us
    pallas_call x1, Pallas kernels, grads(): pl.pallas_call(grad_kernel, grid=(n_loc, parts), in_specs=[part(bm), full...  10.5 us
    ppermute x1, starting transfers between devices, local_step(): from_right = lax.ppermute(left, 'ep', to_left)  1.94 us
    ppermute x1, waiting for transfers between devices, local_step(): from_left = lax.ppermute(right, 'ep', to_right)  1.51 us
  transfers between devices with their start and end apart: 2, of which 1 were waited for; matrix products, arithmetic and copies ran while one was open for 0% of the time, Pallas kernels for 18%

profile of v2, /device:TPU:81, one launch (start us, length us, event | category | flops | bytes accessed | tf_op | source)
XLA Modules:
  0.0 56.7 jit_solution(13780670775956912262)
XLA Ops:
  0.6 40.5 %route.1 = (bf16[4,384,1024]{2,1,0:T(8,128)(2,1)S(1)}, bf16[4,384,1024]{2,1,0:T(8,128)(2,1)S(1)}, bf16[4,384,512]{2,1,0:T(8,128)(2,1)S(1)}, bf16[4,384,512]{2,1,...) custom-call(bf16[128,1024]{1,0:T(8,128)(2,1)} %x_hbm.1, ...), custom_call_target="tpu_custom_call" | custom-call | flops 8053063680 | bytes 14680064 | tf_op jit(solution)/shard_map/route/pallas_call | solution.py:242
  41.1 0.8 %collective-permute-start = (f32[128,1024]{1,0:T(8,128)S(1)}, f32[128,1024]{1,0:T(8,128)S(1)}, u32[]{:S(2)}, u32[]{:S(2)}) collective-permute-start(f32[128,1024]{1,0:T(8,128)S(1)} %get-tuple-element.16), channel_id=1, source_target_pairs={{0,2},{1,3},{2,4},{3,5},{4,6},{5,7},{6,0},{7,1},{8,10},{9,11},{10,... | collective-permute-start | bytes 1572872 | tf_op jit(solution)/shard_map/ppermute | solution.py:330
  42.0 1.9 %collective-permute-start.1 = (f32[128,1024]{1,0:T(8,128)S(1)}, f32[128,1024]{1,0:T(8,128)S(1)}, u32[]{:S(2)}, u32[]{:S(2)}) collective-permute-start(f32[128,1024]{1,0:T(8,128)S(1)} %get-tuple-element.17), channel_id=1, source_target_pairs={{2,0},{3,1},{4,2},{5,3},{6,4},{7,5},{0,6},{1,7},{10,8},{11,9},{12,... | collective-permute-start | bytes 1572872 | tf_op jit(solution)/shard_map/ppermute | solution.py:331
  43.9 10.5 %grads.1 = (f32[4,1024,512]{2,1,0:T(8,128)}, f32[4,512,1024]{2,1,0:T(8,128)}, f32[4,1024,512]{2,1,0:T(8,128)}) custom-call(bf16[4,384,1024]{2,1,0:T(8,128)(2,1)S(1)} %get-tuple-element.18.x_ref, bf16[4,384,1024]{2,1,0:T(8,128)(2,1)S(1)} %get-tuple-element.19.z_ref, bf16[4,384,512]{2,1,0:T(8,128)(2,1)S(1)} %get-tuple-element.20.h_ref, ...), custom_call_target="tpu_custom_call" | custom-call | flops 4831838208 | bytes 27262976 | tf_op jit(solution)/shard_map/grads/pallas_call | solution.py:296
  54.4 1.5 %collective-permute-done = f32[128,1024]{1,0:T(8,128)S(1)} collective-permute-done((f32[128,1024]{1,0:T(8,128)S(1)}, f32[128,1024]{1,0:T(8,128)S(1)}, u32[]{:S(2)}, u32[]{:S(2)}) %collective-permute-start) | collective-permute-done | bytes 524320 | tf_op jit(solution)/shard_map/ppermute | solution.py:330
  55.9 0.0 collective-permute-done.1
  55.9 0.8 %add_convert_fusion = bf16[128,1024]{1,0:T(8,128)(2,1)} fusion(f32[128,1024]{1,0:T(8,128)S(1)} %collective-permute-done.1, f32[128,1024]{1,0:T(8,128)S(1)} %get-tuple-element.15, f32[128,1024]{1,0:T(8,128)S(1)} %collective-permute-done), kind=kLoop, calls=%fused_computation | loop fusion | flops 393216 | bytes 1835008 | tf_op jit(solution)/shard_map/convert_element_type | solution.py:333
Async XLA Ops:
  41.1 14.8 %collective-permute-start = (f32[128,1024]{1,0:T(8,128)S(1)}, f32[128,1024]{1,0:T(8,128)S(1)}, u32[]{:S(2)}, u32[]{:S(2)}) collective-permute-start(f32[128,1024]{1,0:T(8,128)S(1)} %get-tuple-element.16), channel_id=1, source_target_pairs={{0,2},{1,3},{2,4},{3,5},{4,6},{5,7},{6,0},{7,1},{8,10},{9,11},{10,... | collective-permute-start | bytes 1572872 | tf_op jit(solution)/shard_map/ppermute | solution.py:330
  42.0 13.9 %collective-permute-start.1 = (f32[128,1024]{1,0:T(8,128)S(1)}, f32[128,1024]{1,0:T(8,128)S(1)}, u32[]{:S(2)}, u32[]{:S(2)}) collective-permute-start(f32[128,1024]{1,0:T(8,128)S(1)} %get-tuple-element.17), channel_id=1, source_target_pairs={{2,0},{3,1},{4,2},{5,3},{6,4},{7,5},{0,6},{1,7},{10,8},{11,9},{12,... | collective-permute-start | bytes 1572872 | tf_op jit(solution)/shard_map/ppermute | solution.py:331

commit v3 on v2

--- a/solution.py
+++ b/solution.py
@@ -22,12 +22,13 @@
 
 PASSES = (((0, 0), (0, 1)), ((2, 0), (2, 1)), ((1, 0), (1, 1), (3, 0), (3, 1)))
 FIRST = (0, 2, 4)
+LAG = 2
 
 
 def route_kernel(
     n_dev, cap, x_hbm, y_hbm, ids_hbm, slots_hbm, gates_hbm, w1_hbm, w2_hbm, w3_hbm,
     xr, zr, hb, dab, dbb, own_out, right_out, left_out,
-    xb, yb, mb, w1, w2, w3, dxb, oh, part, ddr, hopr, osum, ids, slots, gates,
+    xb, yb, mb, w1, w2, w3, dxb, oht, part, ddr, hopr, osum, ids, slots, gates,
     send_sem, recv_sem, load_sem,
 ):
     n_chip = n_dev // 2
@@ -61,6 +62,8 @@
 
     for c in loads[:2]:
         c.wait()
+    for c in loads[5:]:
+        c.start()
     pl.semaphore_wait(barrier, 3)
 
     made = []
@@ -83,8 +86,6 @@
     y_m = send(yb.at[0, 0], yb.at[0, 1], mate)
     m_r = send(mb.at[0, 0], mb.at[3, 0], right)
     m_l = send(mb.at[0, 0], mb.at[1, 0], left)
-    for c in loads[5:]:
-        c.start()
 
     row_id = lax.broadcasted_iota(jnp.int32, (n_loc * cap, tok), 0) + me * (n_loc * cap)
 
@@ -101,7 +102,7 @@
             gate = jnp.where(hit, gate_of[j:j + 1, :], gate)
         gate_row = jnp.sum(gate, axis=1, keepdims=True)
         hot = hot.astype(BF)
-        oh[q] = hot
+        oht[q] = hot.T
         for n in range(d_model // COLS):
             cols = pl.ds(n * COLS, COLS)
             xv = dot(hot, xb[d, k, :, cols]).astype(BF)
@@ -110,39 +111,40 @@
                 xr[e, pl.ds(q * cap, cap), cols] = xv[e * cap:(e + 1) * cap]
                 zr[e, pl.ds(q * cap, cap), cols] = zv[e * cap:(e + 1) * cap]
 
+    def inner(p, e):
+        at = pl.ds(FIRST[p] * cap, len(PASSES[p]) * cap)
+        x_e = xr[e, at, :]
+        z_e = zr[e, at, :]
+        for n in range(d_ff // COLS):
+            cols = pl.ds(n * COLS, COLS)
+            a = dot(x_e, w1[e, :, cols]).astype(BF).astype(F32)
+            b = dot(x_e, w3[e, :, cols]).astype(BF).astype(F32)
+            dh = dot(z_e, w2[e, cols, :], 1, 1)
+            sg = jax.nn.sigmoid(a)
+            act = a * sg
+            hb[e, at, cols] = (act * b).astype(BF)
+            dab[e, at, cols] = (dh * b * sg * (1.0 + a * (1.0 - sg))).astype(BF)
+            dbb[e, at, cols] = (dh * act).astype(BF)
+
     def experts(p, lo, hi):
+        lax.fori_loop(lo, hi, lambda e, c: (inner(p, e), c)[1], 0)
+
+    def back(p, cols):
         rows = len(PASSES[p]) * cap
         at = pl.ds(FIRST[p] * cap, rows)
 
         def one(e, carry):
-            x_e = xr[e, at, :]
-            z_e = zr[e, at, :]
-            for n in range(d_ff // COLS):
-                cols = pl.ds(n * COLS, COLS)
-                a = dot(x_e, w1[e, :, cols]).astype(BF).astype(F32)
-                b = dot(x_e, w3[e, :, cols]).astype(BF).astype(F32)
-                dh = dot(z_e, w2[e, cols, :], 1, 1)
-                sg = jax.nn.sigmoid(a)
-                act = a * sg
-                hb[e, at, cols] = (act * b).astype(BF)
-                dab[e, at, cols] = (dh * b * sg * (1.0 + a * (1.0 - sg))).astype(BF)
-                dbb[e, at, cols] = (dh * act).astype(BF)
-            da = dab[e, at, :]
-            db = dbb[e, at, :]
-            for n in range(d_model // COLS):
-                cols = pl.ds(n * COLS, COLS)
-                dxb[e, pl.ds(0, rows), cols] = (
-                    dot(da, w1[e, cols, :], 1, 1) + dot(db, w3[e, cols, :], 1, 1)).astype(BF)
+            dxb[e, pl.ds(0, rows), cols] = (
+                dot(dab[e, at, :], w1[e, cols, :], 1, 1) + dot(dbb[e, at, :], w3[e, cols, :], 1, 1)).astype(BF)
             return carry
 
-        lax.fori_loop(lo, hi, one, 0)
-
-    def combine(p, i):
+        for e in range(n_loc):
+            one(e, 0)
+
+    def combine(p, i, cols):
         q = FIRST[p] + i
-        for n in range(d_model // COLS):
-            cols = pl.ds(n * COLS, COLS)
-            back = jnp.concatenate([dxb[e, pl.ds(i * cap, cap), cols] for e in range(n_loc)], axis=0)
-            part[q, :, cols] = dot(oh[q], back, 0, 0)
+        rows = jnp.concatenate([dxb[e, pl.ds(i * cap, cap), cols] for e in range(n_loc)], axis=0)
+        part[q, :, cols] = dot(oht[q], rows)
 
     def forward(i):
         x_r[i].wait_recv()
@@ -150,18 +152,19 @@
         y_l[i].wait_recv()
         y_f.append(send(yb.at[1, 0, halves[i]], yb.at[2, 0, halves[i]], left))
 
+    n_cols = d_model // COLS
+    chunks = [pl.ds(n * COLS, COLS) for n in range(n_cols)]
     x_f, y_f = [], []
     mid = n_loc // 2
     place(0, 0)
-    for c in loads[5:]:
-        c.wait()
     m_m.wait_recv()
     x_m.wait_recv()
     y_m.wait_recv()
     place(0, 1)
+    forward(0)
+    for c in loads[5:]:
+        c.wait()
     experts(0, 0, mid)
-    forward(0)
-    experts(0, mid, n_loc)
     forward(1)
     m_r.wait_recv()
     m_f = send(mb.at[3, 0], mb.at[2, 0], right)
@@ -174,9 +177,15 @@
         send(xb.at[3, 0], xb.at[3, 1], mate),
         send(yb.at[1, 0], yb.at[1, 1], mate),
     ]
-    combine(0, 1)
+    experts(0, mid, n_loc)
+    for cols in chunks:
+        back(0, cols)
+        combine(0, 1, cols)
     d_own = send(part.at[1], ddr.at[0], mate)
-    combine(0, 0)
+    for cols in chunks:
+        combine(0, 0, cols)
+    d_own.wait_recv()
+    own_out[...] = part[0] + ddr[0]
 
     opp = []
     for i, h in enumerate(halves):
@@ -190,21 +199,33 @@
     for c in opp:
         c.wait_recv()
     place(1, 1)
-    experts(1, 0, n_loc - 1)
+    experts(1, 0, n_loc)
+
+    d_opp, hops = [], []
+
+    def hop(n):
+        cols = chunks[n]
+        d_opp[n].wait_recv()
+        osum[:, cols] = part[2, :, cols] + ddr[1, :, cols]
+        hops.append((
+            send(osum.at[pl.ds(0, half), cols], hopr.at[0, :, cols], right),
+            send(osum.at[pl.ds(half, half), cols], hopr.at[1, :, cols], left)))
+
+    for n, cols in enumerate(chunks):
+        back(1, cols)
+        combine(1, 1, cols)
+        d_opp.append(send(part.at[3, :, cols], ddr.at[1, :, cols], mate))
+        combine(1, 0, cols)
+        if n >= LAG:
+            hop(n - LAG)
     y_r.wait_recv()
     y_r2 = send(yb.at[3, 0], yb.at[3, 1], mate)
     x_l.wait_recv()
     x_l2 = send(xb.at[1, 0], xb.at[1, 1], mate)
-    experts(1, n_loc - 1, n_loc)
-    combine(1, 1)
-    d_opp = send(part.at[3], ddr.at[1], mate)
-    combine(1, 0)
+    for n in range(n_cols - LAG, n_cols):
+        hop(n)
     place(2, 0)
     place(2, 2)
-    d_opp.wait_recv()
-    osum[...] = part[2] + ddr[1]
-    hop_r = send(osum.at[pl.ds(0, half)], hopr.at[0], right)
-    hop_l = send(osum.at[pl.ds(half, half)], hopr.at[1], left)
     for c in early:
         c.wait_recv()
     y_r2.wait_recv()
@@ -212,22 +233,34 @@
     place(2, 1)
     place(2, 3)
     experts(2, 0, n_loc)
-    combine(2, 1)
-    d_right = send(part.at[5], ddr.at[2], mate)
-    combine(2, 3)
-    d_left = send(part.at[7], ddr.at[3], mate)
-    combine(2, 0)
-    combine(2, 2)
-    d_own.wait_recv()
-    own_out[...] = part[0] + ddr[0]
-    hop_r.wait_recv()
-    hop_l.wait_recv()
-    part[4, pl.ds(0, half)] += hopr[0]
-    part[6, pl.ds(half, half)] += hopr[1]
-    d_right.wait_recv()
-    right_out[...] = part[4] + ddr[2]
-    d_left.wait_recv()
-    left_out[...] = part[6] + ddr[3]
+
+    d_side = []
+
+    def side(n):
+        cols = chunks[n]
+        for c in d_side[n]:
+            c.wait_recv()
+        for c in hops[n]:
+            c.wait_recv()
+        near, far = pl.ds(0, half), pl.ds(half, half)
+        right_out[near, cols] = part[4, near, cols] + ddr[2, near, cols] + hopr[0, :, cols]
+        right_out[far, cols] = part[4, far, cols] + ddr[2, far, cols]
+        left_out[near, cols] = part[6, near, cols] + ddr[3, near, cols]
+        left_out[far, cols] = part[6, far, cols] + ddr[3, far, cols] + hopr[1, :, cols]
+
+    for n, cols in enumerate(chunks):
+        back(2, cols)
+        combine(2, 1, cols)
+        combine(2, 3, cols)
+        d_side.append((
+            send(part.at[5, :, cols], ddr.at[2, :, cols], mate),
+            send(part.at[7, :, cols], ddr.at[3, :, cols], mate)))
+        combine(2, 0, cols)
+        combine(2, 2, cols)
+        if n >= LAG:
+            side(n - LAG)
+    for n in range(n_cols - LAG, n_cols):
+        side(n)
     for c in made:
         c.wait_send()
 
@@ -261,7 +294,7 @@
             pltpu.VMEM(w2.shape, BF),
             pltpu.VMEM(w3.shape, BF),
             pltpu.VMEM((n_loc, 4 * cap, d_model), BF),
-            pltpu.VMEM((8, n_loc * cap, tok), BF),
+            pltpu.VMEM((8, tok, n_loc * cap), BF),
             pltpu.VMEM((8, tok, d_model), F32),
             pltpu.VMEM((4, tok, d_model), F32),
             pltpu.VMEM((2, tok // 2, d_model), F32),
@@ -269,8 +302,8 @@
             pltpu.VMEM((top_k, tok), jnp.int32),
             pltpu.VMEM((top_k, tok), jnp.int32),
             pltpu.VMEM((top_k, tok), F32),
-            pltpu.SemaphoreType.DMA((40,)),
-            pltpu.SemaphoreType.DMA((40,)),
+            pltpu.SemaphoreType.DMA((56,)),
+            pltpu.SemaphoreType.DMA((56,)),
             pltpu.SemaphoreType.DMA((8,)),
         ],
         compiler_params=pltpu.CompilerParams(

time: 56.8 us -> 56.9 us (level)
  no operation moved by 1% of the time
where the time goes in v3:
time: 56.9 us; the launch traced here: 56.8 us
  Pallas kernels  51.5 us (91%)
  starting transfers between devices  2.76 us (5%)
  waiting for transfers between devices  1.04 us (2%)
  other arithmetic  0.8 us (1%)
  between operations  0.64 us (1%)
    pallas_call x1, Pallas kernels, route(): pl.pallas_call(functools.partial(route_kernel, n_dev, cap), out_shape=(ja...  41.1 us
    pallas_call x1, Pallas kernels, grads(): pl.pallas_call(grad_kernel, grid=(n_loc, parts), in_specs=[part(bm), full...  10.5 us
    ppermute x1, starting transfers between devices, local_step(): from_right = lax.ppermute(left, 'ep', to_left)  1.92 us
  transfers between devices with their start and end apart: 2, of which 1 were waited for; matrix products, arithmetic and copies ran while one was open for 0% of the time, Pallas kernels for 18%

profile of v3, /device:TPU:81, one launch (start us, length us, event | category | flops | bytes accessed | tf_op | source)
XLA Modules:
  0.0 56.8 jit_solution(14941058748884067544)
XLA Ops:
  0.6 41.1 %route.1 = (bf16[4,384,1024]{2,1,0:T(8,128)(2,1)S(1)}, bf16[4,384,1024]{2,1,0:T(8,128)(2,1)S(1)}, bf16[4,384,512]{2,1,0:T(8,128)(2,1)S(1)}, bf16[4,384,512]{2,1,...) custom-call(bf16[128,1024]{1,0:T(8,128)(2,1)} %x_hbm.1, ...), custom_call_target="tpu_custom_call" | custom-call | flops 8053063680 | bytes 14680064 | tf_op jit(solution)/shard_map/route/pallas_call | solution.py:275
  41.7 0.8 %collective-permute-start = (f32[128,1024]{1,0:T(8,128)S(1)}, f32[128,1024]{1,0:T(8,128)S(1)}, u32[]{:S(2)}, u32[]{:S(2)}) collective-permute-start(f32[128,1024]{1,0:T(8,128)S(1)} %get-tuple-element.16), channel_id=1, source_target_pairs={{0,2},{1,3},{2,4},{3,5},{4,6},{5,7},{6,0},{7,1},{8,10},{9,11},{10,... | collective-permute-start | bytes 1572872 | tf_op jit(solution)/shard_map/ppermute | solution.py:363
  42.5 1.9 %collective-permute-start.1 = (f32[128,1024]{1,0:T(8,128)S(1)}, f32[128,1024]{1,0:T(8,128)S(1)}, u32[]{:S(2)}, u32[]{:S(2)}) collective-permute-start(f32[128,1024]{1,0:T(8,128)S(1)} %get-tuple-element.17), channel_id=1, source_target_pairs={{2,0},{3,1},{4,2},{5,3},{6,4},{7,5},{0,6},{1,7},{10,8},{11,9},{12,... | collective-permute-start | bytes 1572872 | tf_op jit(solution)/shard_map/ppermute | solution.py:364
  44.5 10.5 %grads.1 = (f32[4,1024,512]{2,1,0:T(8,128)}, f32[4,512,1024]{2,1,0:T(8,128)}, f32[4,1024,512]{2,1,0:T(8,128)}) custom-call(bf16[4,384,1024]{2,1,0:T(8,128)(2,1)S(1)} %get-tuple-element.18.x_ref, bf16[4,384,1024]{2,1,0:T(8,128)(2,1)S(1)} %get-tuple-element.19.z_ref, bf16[4,384,512]{2,1,0:T(8,128)(2,1)S(1)} %get-tuple-element.20.h_ref, ...), custom_call_target="tpu_custom_call" | custom-call | flops 4831838208 | bytes 27262976 | tf_op jit(solution)/shard_map/grads/pallas_call | solution.py:329
  54.9 1.0 %collective-permute-done = f32[128,1024]{1,0:T(8,128)S(1)} collective-permute-done((f32[128,1024]{1,0:T(8,128)S(1)}, f32[128,1024]{1,0:T(8,128)S(1)}, u32[]{:S(2)}, u32[]{:S(2)}) %collective-permute-start) | collective-permute-done | bytes 524320 | tf_op jit(solution)/shard_map/ppermute | solution.py:363
  56.0 0.0 collective-permute-done.1
  56.0 0.8 %add_convert_fusion = bf16[128,1024]{1,0:T(8,128)(2,1)} fusion(f32[128,1024]{1,0:T(8,128)S(1)} %collective-permute-done.1, f32[128,1024]{1,0:T(8,128)S(1)} %get-tuple-element.15, f32[128,1024]{1,0:T(8,128)S(1)} %collective-permute-done), kind=kLoop, calls=%fused_computation | loop fusion | flops 393216 | bytes 1835008 | tf_op jit(solution)/shard_map/convert_element_type | solution.py:366
Async XLA Ops:
  41.7 14.3 %collective-permute-start = (f32[128,1024]{1,0:T(8,128)S(1)}, f32[128,1024]{1,0:T(8,128)S(1)}, u32[]{:S(2)}, u32[]{:S(2)}) collective-permute-start(f32[128,1024]{1,0:T(8,128)S(1)} %get-tuple-element.16), channel_id=1, source_target_pairs={{0,2},{1,3},{2,4},{3,5},{4,6},{5,7},{6,0},{7,1},{8,10},{9,11},{10,... | collective-permute-start | bytes 1572872 | tf_op jit(solution)/shard_map/ppermute | solution.py:363
  42.5 13.4 %collective-permute-start.1 = (f32[128,1024]{1,0:T(8,128)S(1)}, f32[128,1024]{1,0:T(8,128)S(1)}, u32[]{:S(2)}, u32[]{:S(2)}) collective-permute-start(f32[128,1024]{1,0:T(8,128)S(1)} %get-tuple-element.17), channel_id=1, source_target_pairs={{2,0},{3,1},{4,2},{5,3},{6,4},{7,5},{0,6},{1,7},{10,8},{11,9},{12,... | collective-permute-start | bytes 1572872 | tf_op jit(solution)/shard_map/ppermute | solution.py:364

commit v4 on v3

--- a/solution.py
+++ b/solution.py
@@ -28,7 +28,7 @@
 def route_kernel(
     n_dev, cap, x_hbm, y_hbm, ids_hbm, slots_hbm, gates_hbm, w1_hbm, w2_hbm, w3_hbm,
     xr, zr, hb, dab, dbb, own_out, right_out, left_out,
-    xb, yb, mb, w1, w2, w3, dxb, oht, part, ddr, hopr, osum, ids, slots, gates,
+    xb, yb, mb, w1, w2, w3, w1t, w2t, w3t, dxb, oht, part, ddr, hopr, osum, ids, slots, gates,
     send_sem, recv_sem, load_sem,
 ):
     n_chip = n_dev // 2
@@ -46,7 +46,7 @@
         pltpu.make_async_copy(src, dst, load_sem.at[i])
         for i, (src, dst) in enumerate((
             (x_hbm, xb.at[0, 0]), (y_hbm, yb.at[0, 0]), (ids_hbm, ids), (slots_hbm, slots), (gates_hbm, gates),
-            (w1_hbm, w1), (w3_hbm, w3), (w2_hbm, w2)))
+            (w2_hbm, w2), (w1_hbm, w1), (w3_hbm, w3)))
     ]
     for c in loads[:5]:
         c.start()
@@ -111,6 +111,15 @@
                 xr[e, pl.ds(q * cap, cap), cols] = xv[e * cap:(e + 1) * cap]
                 zr[e, pl.ds(q * cap, cap), cols] = zv[e * cap:(e + 1) * cap]
 
+    def turn(src, dst):
+        def one(e, carry):
+            for n in range(src.shape[1] // COLS):
+                cols = pl.ds(n * COLS, COLS)
+                dst[e, :, cols] = src[e, cols, :].T
+            return carry
+
+        lax.fori_loop(0, n_loc, one, 0)
+
     def inner(p, e):
         at = pl.ds(FIRST[p] * cap, len(PASSES[p]) * cap)
         x_e = xr[e, at, :]
@@ -119,7 +128,7 @@
             cols = pl.ds(n * COLS, COLS)
             a = dot(x_e, w1[e, :, cols]).astype(BF).astype(F32)
             b = dot(x_e, w3[e, :, cols]).astype(BF).astype(F32)
-            dh = dot(z_e, w2[e, cols, :], 1, 1)
+            dh = dot(z_e, w2t[e, :, cols])
             sg = jax.nn.sigmoid(a)
             act = a * sg
             hb[e, at, cols] = (act * b).astype(BF)
@@ -135,7 +144,7 @@
 
         def one(e, carry):
             dxb[e, pl.ds(0, rows), cols] = (
-                dot(dab[e, at, :], w1[e, cols, :], 1, 1) + dot(dbb[e, at, :], w3[e, cols, :], 1, 1)).astype(BF)
+                dot(dab[e, at, :], w1t[e, :, cols]) + dot(dbb[e, at, :], w3t[e, :, cols])).astype(BF)
             return carry
 
         for e in range(n_loc):
@@ -155,16 +164,18 @@
     n_cols = d_model // COLS
     chunks = [pl.ds(n * COLS, COLS) for n in range(n_cols)]
     x_f, y_f = [], []
-    mid = n_loc // 2
     place(0, 0)
+    loads[5].wait()
+    turn(w2, w2t)
     m_m.wait_recv()
     x_m.wait_recv()
     y_m.wait_recv()
     place(0, 1)
     forward(0)
-    for c in loads[5:]:
-        c.wait()
-    experts(0, 0, mid)
+    loads[6].wait()
+    turn(w1, w1t)
+    loads[7].wait()
+    turn(w3, w3t)
     forward(1)
     m_r.wait_recv()
     m_f = send(mb.at[3, 0], mb.at[2, 0], right)
@@ -177,7 +188,7 @@
         send(xb.at[3, 0], xb.at[3, 1], mate),
         send(yb.at[1, 0], yb.at[1, 1], mate),
     ]
-    experts(0, mid, n_loc)
+    experts(0, 0, n_loc)
     for cols in chunks:
         back(0, cols)
         combine(0, 1, cols)
@@ -293,6 +304,9 @@
             pltpu.VMEM(w1.shape, BF),
             pltpu.VMEM(w2.shape, BF),
             pltpu.VMEM(w3.shape, BF),
+            pltpu.VMEM(w2.shape, BF),
+            pltpu.VMEM(w1.shape, BF),
+            pltpu.VMEM(w2.shape, BF),
             pltpu.VMEM((n_loc, 4 * cap, d_model), BF),
             pltpu.VMEM((8, tok, n_loc * cap), BF),
             pltpu.VMEM((8, tok, d_model), F32),
@@ -307,7 +321,7 @@
             pltpu.SemaphoreType.DMA((8,)),
         ],
         compiler_params=pltpu.CompilerParams(
-            collective_id=0, has_side_effects=True, vmem_limit_bytes=36 * 1024 * 1024),
+            collective_id=0, has_side_effects=True, vmem_limit_bytes=41 * 1024 * 1024),
         cost_estimate=pl.CostEstimate(flops=flops, bytes_accessed=14 * 1024 * 1024, transcendentals=0),
         name="route",
     )(*(pltpu.with_memory_space_constraint(v, pltpu.HBM) for v in (x, y, ids, slots, gates, w1, w2, w3)))

time: 56.9 us -> 53.8 us (0.946)
  Pallas kernels: 51.5 us -> 48.4 us
    pallas_call x1, Pallas kernels: 41.1 us -> 37.9 us  [route(): pl.pallas_call(functools.partial(route_kernel, n_dev, cap), out_shape=(ja...]
  transfers between devices with their start and end apart: 2 -> 2, of which waited for: 1 -> 1; matrix products, arithmetic and copies ran while one was open for 0% -> 0% of each run, Pallas kernels for 18% -> 20%
where the time goes in v4:
time: 53.8 us; the launch traced here: 53.7 us
  Pallas kernels  48.4 us (90%)
  starting transfers between devices  2.76 us (5%)
  waiting for transfers between devices  1.04 us (2%)
  other arithmetic  0.8 us (1%)
  between operations  0.64 us (1%)
    pallas_call x1, Pallas kernels, route(): pl.pallas_call(functools.partial(route_kernel, n_dev, cap), out_shape=(ja...  37.9 us
    pallas_call x1, Pallas kernels, grads(): pl.pallas_call(grad_kernel, grid=(n_loc, parts), in_specs=[part(bm), full...  10.5 us
    ppermute x1, starting transfers between devices, local_step(): from_right = lax.ppermute(left, 'ep', to_left)  1.93 us
  transfers between devices with their start and end apart: 2, of which 1 were waited for; matrix products, arithmetic and copies ran while one was open for 0% of the time, Pallas kernels for 20%

profile of v4, /device:TPU:81, one launch (start us, length us, event | category | flops | bytes accessed | tf_op | source)
XLA Modules:
  0.0 53.7 jit_solution(16950272823471858120)
XLA Ops:
  0.6 37.9 %route.1 = (bf16[4,384,1024]{2,1,0:T(8,128)(2,1)S(1)}, bf16[4,384,1024]{2,1,0:T(8,128)(2,1)S(1)}, bf16[4,384,512]{2,1,0:T(8,128)(2,1)S(1)}, bf16[4,384,512]{2,1,...) custom-call(bf16[128,1024]{1,0:T(8,128)(2,1)} %x_hbm.1, ...), custom_call_target="tpu_custom_call" | custom-call | flops 8053063680 | bytes 14680064 | tf_op jit(solution)/shard_map/route/pallas_call | solution.py:286
  38.6 0.8 %collective-permute-start = (f32[128,1024]{1,0:T(8,128)S(1)}, f32[128,1024]{1,0:T(8,128)S(1)}, u32[]{:S(2)}, u32[]{:S(2)}) collective-permute-start(f32[128,1024]{1,0:T(8,128)S(1)} %get-tuple-element.16), channel_id=1, source_target_pairs={{0,2},{1,3},{2,4},{3,5},{4,6},{5,7},{6,0},{7,1},{8,10},{9,11},{10,... | collective-permute-start | bytes 1572872 | tf_op jit(solution)/shard_map/ppermute | solution.py:377
  39.4 1.9 %collective-permute-start.1 = (f32[128,1024]{1,0:T(8,128)S(1)}, f32[128,1024]{1,0:T(8,128)S(1)}, u32[]{:S(2)}, u32[]{:S(2)}) collective-permute-start(f32[128,1024]{1,0:T(8,128)S(1)} %get-tuple-element.17), channel_id=1, source_target_pairs={{2,0},{3,1},{4,2},{5,3},{6,4},{7,5},{0,6},{1,7},{10,8},{11,9},{12,... | collective-permute-start | bytes 1572872 | tf_op jit(solution)/shard_map/ppermute | solution.py:378
  41.3 10.5 %grads.1 = (f32[4,1024,512]{2,1,0:T(8,128)}, f32[4,512,1024]{2,1,0:T(8,128)}, f32[4,1024,512]{2,1,0:T(8,128)}) custom-call(bf16[4,384,1024]{2,1,0:T(8,128)(2,1)S(1)} %get-tuple-element.18.x_ref, bf16[4,384,1024]{2,1,0:T(8,128)(2,1)S(1)} %get-tuple-element.19.z_ref, bf16[4,384,512]{2,1,0:T(8,128)(2,1)S(1)} %get-tuple-element.20.h_ref, ...), custom_call_target="tpu_custom_call" | custom-call | flops 4831838208 | bytes 27262976 | tf_op jit(solution)/shard_map/grads/pallas_call | solution.py:343
  51.8 1.0 %collective-permute-done = f32[128,1024]{1,0:T(8,128)S(1)} collective-permute-done((f32[128,1024]{1,0:T(8,128)S(1)}, f32[128,1024]{1,0:T(8,128)S(1)}, u32[]{:S(2)}, u32[]{:S(2)}) %collective-permute-start) | collective-permute-done | bytes 524320 | tf_op jit(solution)/shard_map/ppermute | solution.py:377
  52.9 0.0 collective-permute-done.1
  52.9 0.8 %add_convert_fusion = bf16[128,1024]{1,0:T(8,128)(2,1)} fusion(f32[128,1024]{1,0:T(8,128)S(1)} %collective-permute-done.1, f32[128,1024]{1,0:T(8,128)S(1)} %get-tuple-element.15, f32[128,1024]{1,0:T(8,128)S(1)} %collective-permute-done), kind=kLoop, calls=%fused_computation | loop fusion | flops 393216 | bytes 1835008 | tf_op jit(solution)/shard_map/convert_element_type | solution.py:380
Async XLA Ops:
  38.6 14.3 %collective-permute-start = (f32[128,1024]{1,0:T(8,128)S(1)}, f32[128,1024]{1,0:T(8,128)S(1)}, u32[]{:S(2)}, u32[]{:S(2)}) collective-permute-start(f32[128,1024]{1,0:T(8,128)S(1)} %get-tuple-element.16), channel_id=1, source_target_pairs={{0,2},{1,3},{2,4},{3,5},{4,6},{5,7},{6,0},{7,1},{8,10},{9,11},{10,... | collective-permute-start | bytes 1572872 | tf_op jit(solution)/shard_map/ppermute | solution.py:377
  39.4 13.4 %collective-permute-start.1 = (f32[128,1024]{1,0:T(8,128)S(1)}, f32[128,1024]{1,0:T(8,128)S(1)}, u32[]{:S(2)}, u32[]{:S(2)}) collective-permute-start(f32[128,1024]{1,0:T(8,128)S(1)} %get-tuple-element.17), channel_id=1, source_target_pairs={{2,0},{3,1},{4,2},{5,3},{6,4},{7,5},{0,6},{1,7},{10,8},{11,9},{12,... | collective-permute-start | bytes 1572872 | tf_op jit(solution)/shard_map/ppermute | solution.py:378

commit v5 on v4

--- a/solution.py
+++ b/solution.py
@@ -28,7 +28,7 @@
 def route_kernel(
     n_dev, cap, x_hbm, y_hbm, ids_hbm, slots_hbm, gates_hbm, w1_hbm, w2_hbm, w3_hbm,
     xr, zr, hb, dab, dbb, own_out, right_out, left_out,
-    xb, yb, mb, w1, w2, w3, w1t, w2t, w3t, dxb, oht, part, ddr, hopr, osum, ids, slots, gates,
+    xb, yb, mb, w1, w2, w3, w1t, w2t, w3t, dxb, oh, oht, gr, part, ddr, hopr, osum, ids, slots, gates,
     send_sem, recv_sem, load_sem,
 ):
     n_chip = n_dev // 2
@@ -89,7 +89,7 @@
 
     row_id = lax.broadcasted_iota(jnp.int32, (n_loc * cap, tok), 0) + me * (n_loc * cap)
 
-    def place(p, i):
+    def mask(p, i):
         d, k = PASSES[p][i]
         q = FIRST[p] + i
         keys = mb[d, k, 0:top_k, :].astype(jnp.int32)
@@ -100,16 +100,35 @@
             hit = keys[j:j + 1, :] == row_id
             hot = jnp.where(hit, 1.0, hot)
             gate = jnp.where(hit, gate_of[j:j + 1, :], gate)
-        gate_row = jnp.sum(gate, axis=1, keepdims=True)
         hot = hot.astype(BF)
+        oh[q] = hot
         oht[q] = hot.T
+        gr[q] = jnp.broadcast_to(jnp.sum(gate, axis=1, keepdims=True), gate.shape)
+
+    def place_x(p, i):
+        d, k = PASSES[p][i]
+        q = FIRST[p] + i
+        hot = oh[q]
         for n in range(d_model // COLS):
             cols = pl.ds(n * COLS, COLS)
             xv = dot(hot, xb[d, k, :, cols]).astype(BF)
+            for e in range(n_loc):
+                xr[e, pl.ds(q * cap, cap), cols] = xv[e * cap:(e + 1) * cap]
+
+    def place_z(p, i):
+        d, k = PASSES[p][i]
+        q = FIRST[p] + i
+        hot = oh[q]
+        gate_row = jnp.concatenate([gr[q]] * (COLS // tok), axis=1)
+        for n in range(d_model // COLS):
+            cols = pl.ds(n * COLS, COLS)
             zv = (dot(hot, yb[d, k, :, cols]) * gate_row).astype(BF)
             for e in range(n_loc):
-                xr[e, pl.ds(q * cap, cap), cols] = xv[e * cap:(e + 1) * cap]
                 zr[e, pl.ds(q * cap, cap), cols] = zv[e * cap:(e + 1) * cap]
+
+    def place(p, i):
+        place_x(p, i)
+        place_z(p, i)
 
     def turn(src, dst):
         def one(e, carry):
@@ -150,10 +169,12 @@
         for e in range(n_loc):
             one(e, 0)
 
+    sums = (own_out, part.at[0], osum, part.at[1], right_out, part.at[2], left_out, part.at[3])
+
     def combine(p, i, cols):
         q = FIRST[p] + i
         rows = jnp.concatenate([dxb[e, pl.ds(i * cap, cap), cols] for e in range(n_loc)], axis=0)
-        part[q, :, cols] = dot(oht[q], rows)
+        sums[q][:, cols] = dot(oht[q], rows)
 
     def forward(i):
         x_r[i].wait_recv()
@@ -164,10 +185,12 @@
     n_cols = d_model // COLS
     chunks = [pl.ds(n * COLS, COLS) for n in range(n_cols)]
     x_f, y_f = [], []
+    mask(0, 0)
     place(0, 0)
     loads[5].wait()
     turn(w2, w2t)
     m_m.wait_recv()
+    mask(0, 1)
     x_m.wait_recv()
     y_m.wait_recv()
     place(0, 1)
@@ -192,11 +215,20 @@
     for cols in chunks:
         back(0, cols)
         combine(0, 1, cols)
-    d_own = send(part.at[1], ddr.at[0], mate)
+    d_own = send(sums[1], ddr.at[0], mate)
     for cols in chunks:
         combine(0, 0, cols)
     d_own.wait_recv()
-    own_out[...] = part[0] + ddr[0]
+    own_out[...] += ddr[0]
+    for i in range(2):
+        early[i].wait_recv()
+    for i in range(4):
+        mask(2, i)
+    place_z(2, 0)
+    place_x(2, 2)
+    m_f.wait_recv()
+    m_f2 = send(mb.at[2, 0], mb.at[2, 1], mate)
+    mask(1, 0)
 
     opp = []
     for i, h in enumerate(halves):
@@ -204,8 +236,8 @@
         opp.append(send(xb.at[2, 0, h], xb.at[2, 1, h], mate))
         y_f[i].wait_recv()
         opp.append(send(yb.at[2, 0, h], yb.at[2, 1, h], mate))
-    m_f.wait_recv()
-    opp.append(send(mb.at[2, 0], mb.at[2, 1], mate))
+    m_f2.wait_recv()
+    mask(1, 1)
     place(1, 0)
     for c in opp:
         c.wait_recv()
@@ -217,7 +249,7 @@
     def hop(n):
         cols = chunks[n]
         d_opp[n].wait_recv()
-        osum[:, cols] = part[2, :, cols] + ddr[1, :, cols]
+        osum[:, cols] += ddr[1, :, cols]
         hops.append((
             send(osum.at[pl.ds(0, half), cols], hopr.at[0, :, cols], right),
             send(osum.at[pl.ds(half, half), cols], hopr.at[1, :, cols], left)))
@@ -225,7 +257,7 @@
     for n, cols in enumerate(chunks):
         back(1, cols)
         combine(1, 1, cols)
-        d_opp.append(send(part.at[3, :, cols], ddr.at[1, :, cols], mate))
+        d_opp.append(send(sums[3].at[:, cols], ddr.at[1, :, cols], mate))
         combine(1, 0, cols)
         if n >= LAG:
             hop(n - LAG)
@@ -235,14 +267,16 @@
     x_l2 = send(xb.at[1, 0], xb.at[1, 1], mate)
     for n in range(n_cols - LAG, n_cols):
         hop(n)
-    place(2, 0)
-    place(2, 2)
-    for c in early:
+    for c in early[2:]:
         c.wait_recv()
+    place_z(2, 1)
+    place_x(2, 3)
+    place_x(2, 0)
+    place_z(2, 2)
     y_r2.wait_recv()
     x_l2.wait_recv()
-    place(2, 1)
-    place(2, 3)
+    place_x(2, 1)
+    place_z(2, 3)
     experts(2, 0, n_loc)
 
     d_side = []
@@ -254,18 +288,18 @@
         for c in hops[n]:
             c.wait_recv()
         near, far = pl.ds(0, half), pl.ds(half, half)
-        right_out[near, cols] = part[4, near, cols] + ddr[2, near, cols] + hopr[0, :, cols]
-        right_out[far, cols] = part[4, far, cols] + ddr[2, far, cols]
-        left_out[near, cols] = part[6, near, cols] + ddr[3, near, cols]
-        left_out[far, cols] = part[6, far, cols] + ddr[3, far, cols] + hopr[1, :, cols]
+        right_out[near, cols] += ddr[2, near, cols] + hopr[0, :, cols]
+        right_out[far, cols] += ddr[2, far, cols]
+        left_out[near, cols] += ddr[3, near, cols]
+        left_out[far, cols] += ddr[3, far, cols] + hopr[1, :, cols]
 
     for n, cols in enumerate(chunks):
         back(2, cols)
         combine(2, 1, cols)
         combine(2, 3, cols)
         d_side.append((
-            send(part.at[5, :, cols], ddr.at[2, :, cols], mate),
-            send(part.at[7, :, cols], ddr.at[3, :, cols], mate)))
+            send(sums[5].at[:, cols], ddr.at[2, :, cols], mate),
+            send(sums[7].at[:, cols], ddr.at[3, :, cols], mate)))
         combine(2, 0, cols)
         combine(2, 2, cols)
         if n >= LAG:
@@ -308,8 +342,10 @@
             pltpu.VMEM(w1.shape, BF),
             pltpu.VMEM(w2.shape, BF),
             pltpu.VMEM((n_loc, 4 * cap, d_model), BF),
+            pltpu.VMEM((8, n_loc * cap, tok), BF),
             pltpu.VMEM((8, tok, n_loc * cap), BF),
-            pltpu.VMEM((8, tok, d_model), F32),
+            pltpu.VMEM((8, n_loc * cap, tok), F32),
+            pltpu.VMEM((4, tok, d_model), F32),
             pltpu.VMEM((4, tok, d_model), F32),
             pltpu.VMEM((2, tok // 2, d_model), F32),
             pltpu.VMEM((tok, d_model), F32),
@@ -321,7 +357,7 @@
             pltpu.SemaphoreType.DMA((8,)),
         ],
         compiler_params=pltpu.CompilerParams(
-            collective_id=0, has_side_effects=True, vmem_limit_bytes=41 * 1024 * 1024),
+            collective_id=0, has_side_effects=True, vmem_limit_bytes=42000000),
         cost_estimate=pl.CostEstimate(flops=flops, bytes_accessed=14 * 1024 * 1024, transcendentals=0),
         name="route",
     )(*(pltpu.with_memory_space_constraint(v, pltpu.HBM) for v in (x, y, ids, slots, gates, w1, w2, w3)))

time: 53.8 us -> 54.3 us (level)
  transfers between devices with their start and end apart: 2 -> 2, of which waited for: 1 -> 1; matrix products, arithmetic and copies ran while one was open for 0% -> 0% of each run, Pallas kernels for 20% -> 19%
where the time goes in v5:
time: 54.3 us; the launch traced here: 54.2 us
  Pallas kernels  48.9 us (90%)
  starting transfers between devices  2.76 us (5%)
  waiting for transfers between devices  1.04 us (2%)
  other arithmetic  0.81 us (1%)
  between operations  0.64 us (1%)
    pallas_call x1, Pallas kernels, route(): pl.pallas_call(functools.partial(route_kernel, n_dev, cap), out_shape=(ja...  38.4 us
    pallas_call x1, Pallas kernels, grads(): pl.pallas_call(grad_kernel, grid=(n_loc, parts), in_specs=[part(bm), full...  10.5 us
    ppermute x1, starting transfers between devices, local_step(): from_right = lax.ppermute(left, 'ep', to_left)  1.91 us
  transfers between devices with their start and end apart: 2, of which 1 were waited for; matrix products, arithmetic and copies ran while one was open for 0% of the time, Pallas kernels for 19%

profile of v5, /device:TPU:81, one launch (start us, length us, event | category | flops | bytes accessed | tf_op | source)
XLA Modules:
  0.0 54.2 jit_solution(15411673192438364963)
XLA Ops:
  0.6 38.4 %route.1 = (bf16[4,384,1024]{2,1,0:T(8,128)(2,1)S(1)}, bf16[4,384,1024]{2,1,0:T(8,128)(2,1)S(1)}, bf16[4,384,512]{2,1,0:T(8,128)(2,1)S(1)}, bf16[4,384,512]{2,1,...) custom-call(bf16[128,1024]{1,0:T(8,128)(2,1)} %x_hbm.1, ...), custom_call_target="tpu_custom_call" | custom-call | flops 8053063680 | bytes 14680064 | tf_op jit(solution)/shard_map/route/pallas_call | solution.py:320
  39.1 0.9 %collective-permute-start = (f32[128,1024]{1,0:T(8,128)S(1)}, f32[128,1024]{1,0:T(8,128)S(1)}, u32[]{:S(2)}, u32[]{:S(2)}) collective-permute-start(f32[128,1024]{1,0:T(8,128)S(1)} %get-tuple-element.16), channel_id=1, source_target_pairs={{0,2},{1,3},{2,4},{3,5},{4,6},{5,7},{6,0},{7,1},{8,10},{9,11},{10,... | collective-permute-start | bytes 1572872 | tf_op jit(solution)/shard_map/ppermute | solution.py:413
  39.9 1.9 %collective-permute-start.1 = (f32[128,1024]{1,0:T(8,128)S(1)}, f32[128,1024]{1,0:T(8,128)S(1)}, u32[]{:S(2)}, u32[]{:S(2)}) collective-permute-start(f32[128,1024]{1,0:T(8,128)S(1)} %get-tuple-element.17), channel_id=1, source_target_pairs={{2,0},{3,1},{4,2},{5,3},{6,4},{7,5},{0,6},{1,7},{10,8},{11,9},{12,... | collective-permute-start | bytes 1572872 | tf_op jit(solution)/shard_map/ppermute | solution.py:414
  41.8 10.5 %grads.1 = (f32[4,1024,512]{2,1,0:T(8,128)}, f32[4,512,1024]{2,1,0:T(8,128)}, f32[4,1024,512]{2,1,0:T(8,128)}) custom-call(bf16[4,384,1024]{2,1,0:T(8,128)(2,1)S(1)} %get-tuple-element.18.x_ref, bf16[4,384,1024]{2,1,0:T(8,128)(2,1)S(1)} %get-tuple-element.19.z_ref, bf16[4,384,512]{2,1,0:T(8,128)(2,1)S(1)} %get-tuple-element.20.h_ref, ...), custom_call_target="tpu_custom_call" | custom-call | flops 4831838208 | bytes 27262976 | tf_op jit(solution)/shard_map/grads/pallas_call | solution.py:379
  52.3 1.0 %collective-permute-done = f32[128,1024]{1,0:T(8,128)S(1)} collective-permute-done((f32[128,1024]{1,0:T(8,128)S(1)}, f32[128,1024]{1,0:T(8,128)S(1)}, u32[]{:S(2)}, u32[]{:S(2)}) %collective-permute-start) | collective-permute-done | bytes 524320 | tf_op jit(solution)/shard_map/ppermute | solution.py:413
  53.4 0.0 collective-permute-done.1
  53.4 0.8 %add_convert_fusion = bf16[128,1024]{1,0:T(8,128)(2,1)} fusion(f32[128,1024]{1,0:T(8,128)S(1)} %collective-permute-done.1, f32[128,1024]{1,0:T(8,128)S(1)} %get-tuple-element.15, f32[128,1024]{1,0:T(8,128)S(1)} %collective-permute-done), kind=kLoop, calls=%fused_computation | loop fusion | flops 393216 | bytes 1835008 | tf_op jit(solution)/shard_map/convert_element_type | solution.py:416
Async XLA Ops:
  39.1 14.3 %collective-permute-start = (f32[128,1024]{1,0:T(8,128)S(1)}, f32[128,1024]{1,0:T(8,128)S(1)}, u32[]{:S(2)}, u32[]{:S(2)}) collective-permute-start(f32[128,1024]{1,0:T(8,128)S(1)} %get-tuple-element.16), channel_id=1, source_target_pairs={{0,2},{1,3},{2,4},{3,5},{4,6},{5,7},{6,0},{7,1},{8,10},{9,11},{10,... | collective-permute-start | bytes 1572872 | tf_op jit(solution)/shard_map/ppermute | solution.py:413
  39.9 13.4 %collective-permute-start.1 = (f32[128,1024]{1,0:T(8,128)S(1)}, f32[128,1024]{1,0:T(8,128)S(1)}, u32[]{:S(2)}, u32[]{:S(2)}) collective-permute-start(f32[128,1024]{1,0:T(8,128)S(1)} %get-tuple-element.17), channel_id=1, source_target_pairs={{2,0},{3,1},{4,2},{5,3},{6,4},{7,5},{0,6},{1,7},{10,8},{11,9},{12,... | collective-permute-start | bytes 1572872 | tf_op jit(solution)/shard_map/ppermute | solution.py:414

commit v6 on v5

--- a/solution.py
+++ b/solution.py
@@ -218,8 +218,6 @@
     d_own = send(sums[1], ddr.at[0], mate)
     for cols in chunks:
         combine(0, 0, cols)
-    d_own.wait_recv()
-    own_out[...] += ddr[0]
     for i in range(2):
         early[i].wait_recv()
     for i in range(4):
@@ -261,17 +259,18 @@
         combine(1, 0, cols)
         if n >= LAG:
             hop(n - LAG)
-    y_r.wait_recv()
-    y_r2 = send(yb.at[3, 0], yb.at[3, 1], mate)
-    x_l.wait_recv()
-    x_l2 = send(xb.at[1, 0], xb.at[1, 1], mate)
-    for n in range(n_cols - LAG, n_cols):
-        hop(n)
+        if n == 1:
+            y_r.wait_recv()
+            y_r2 = send(yb.at[3, 0], yb.at[3, 1], mate)
+            x_l.wait_recv()
+            x_l2 = send(xb.at[1, 0], xb.at[1, 1], mate)
     for c in early[2:]:
         c.wait_recv()
     place_z(2, 1)
+    hop(n_cols - 2)
     place_x(2, 3)
     place_x(2, 0)
+    hop(n_cols - 1)
     place_z(2, 2)
     y_r2.wait_recv()
     x_l2.wait_recv()
@@ -304,6 +303,8 @@
         combine(2, 2, cols)
         if n >= LAG:
             side(n - LAG)
+    d_own.wait_recv()
+    own_out[...] += ddr[0]
     for n in range(n_cols - LAG, n_cols):
         side(n)
     for c in made:

time: 54.3 us -> 54.3 us (level)
    ppermute x1, starting transfers between devices: 0.85 us -> 0.11 us  [local_step(): from_left = lax.ppermute(right, 'ep', to_right)]
    ppermute x1, starting transfers between devices: 1.91 us -> 2.65 us  [local_step(): from_right = lax.ppermute(left, 'ep', to_left)]
where the time goes in v6:
time: 54.3 us; the launch traced here: 54.2 us
  Pallas kernels  48.5 us (89%)
  starting transfers between devices  2.76 us (5%)
  waiting for transfers between devices  1.48 us (3%)
  other arithmetic  0.81 us (1%)
  between operations  0.65 us (1%)
    pallas_call x1, Pallas kernels, route(): pl.pallas_call(functools.partial(route_kernel, n_dev, cap), out_shape=(ja...  38 us
    pallas_call x1, Pallas kernels, grads(): pl.pallas_call(grad_kernel, grid=(n_loc, parts), in_specs=[part(bm), full...  10.5 us
    ppermute x1, starting transfers between devices, local_step(): from_right = lax.ppermute(left, 'ep', to_left)  2.65 us
    ppermute x1, waiting for transfers between devices, local_step(): from_left = lax.ppermute(right, 'ep', to_right)  1.48 us
  transfers between devices with their start and end apart: 2, of which 1 were waited for; matrix products, arithmetic and copies ran while one was open for 0% of the time, Pallas kernels for 19%

profile of v6, /device:TPU:81, one launch (start us, length us, event | category | flops | bytes accessed | tf_op | source)
XLA Modules:
  0.0 54.2 jit_solution(15520765825307946695)
XLA Ops:
  0.6 38.0 %route.1 = (bf16[4,384,1024]{2,1,0:T(8,128)(2,1)S(1)}, bf16[4,384,1024]{2,1,0:T(8,128)(2,1)S(1)}, bf16[4,384,512]{2,1,0:T(8,128)(2,1)S(1)}, bf16[4,384,512]{2,1,...) custom-call(bf16[128,1024]{1,0:T(8,128)(2,1)} %x_hbm.1, ...), custom_call_target="tpu_custom_call" | custom-call | flops 8053063680 | bytes 14680064 | tf_op jit(solution)/shard_map/route/pallas_call | solution.py:321
  38.6 0.1 collective-permute-start
  38.8 2.6 %collective-permute-start.1 = (f32[128,1024]{1,0:T(8,128)S(1)}, f32[128,1024]{1,0:T(8,128)S(1)}, u32[]{:S(2)}, u32[]{:S(2)}) collective-permute-start(f32[128,1024]{1,0:T(8,128)S(1)} %get-tuple-element.17), channel_id=1, source_target_pairs={{2,0},{3,1},{4,2},{5,3},{6,4},{7,5},{0,6},{1,7},{10,8},{11,9},{12,... | collective-permute-start | bytes 1572872 | tf_op jit(solution)/shard_map/ppermute | solution.py:415
  41.4 10.5 %grads.1 = (f32[4,1024,512]{2,1,0:T(8,128)}, f32[4,512,1024]{2,1,0:T(8,128)}, f32[4,1024,512]{2,1,0:T(8,128)}) custom-call(bf16[4,384,1024]{2,1,0:T(8,128)(2,1)S(1)} %get-tuple-element.18.x_ref, bf16[4,384,1024]{2,1,0:T(8,128)(2,1)S(1)} %get-tuple-element.19.z_ref, bf16[4,384,512]{2,1,0:T(8,128)(2,1)S(1)} %get-tuple-element.20.h_ref, ...), custom_call_target="tpu_custom_call" | custom-call | flops 4831838208 | bytes 27262976 | tf_op jit(solution)/shard_map/grads/pallas_call | solution.py:380
  51.9 1.5 %collective-permute-done = f32[128,1024]{1,0:T(8,128)S(1)} collective-permute-done((f32[128,1024]{1,0:T(8,128)S(1)}, f32[128,1024]{1,0:T(8,128)S(1)}, u32[]{:S(2)}, u32[]{:S(2)}) %collective-permute-start) | collective-permute-done | bytes 524320 | tf_op jit(solution)/shard_map/ppermute | solution.py:414
  53.4 0.0 collective-permute-done.1
  53.4 0.8 %add_convert_fusion = bf16[128,1024]{1,0:T(8,128)(2,1)} fusion(f32[128,1024]{1,0:T(8,128)S(1)} %collective-permute-done.1, f32[128,1024]{1,0:T(8,128)S(1)} %get-tuple-element.15, f32[128,1024]{1,0:T(8,128)S(1)} %collective-permute-done), kind=kLoop, calls=%fused_computation | loop fusion | flops 393216 | bytes 1835008 | tf_op jit(solution)/shard_map/convert_element_type | solution.py:417
Async XLA Ops:
  38.6 14.7 %collective-permute-start = (f32[128,1024]{1,0:T(8,128)S(1)}, f32[128,1024]{1,0:T(8,128)S(1)}, u32[]{:S(2)}, u32[]{:S(2)}) collective-permute-start(f32[128,1024]{1,0:T(8,128)S(1)} %get-tuple-element.16), channel_id=1, source_target_pairs={{0,2},{1,3},{2,4},{3,5},{4,6},{5,7},{6,0},{7,1},{8,10},{9,11},{10,... | collective-permute-start | bytes 1572872 | tf_op jit(solution)/shard_map/ppermute | solution.py:414
  38.8 14.6 %collective-permute-start.1 = (f32[128,1024]{1,0:T(8,128)S(1)}, f32[128,1024]{1,0:T(8,128)S(1)}, u32[]{:S(2)}, u32[]{:S(2)}) collective-permute-start(f32[128,1024]{1,0:T(8,128)S(1)} %get-tuple-element.17), channel_id=1, source_target_pairs={{2,0},{3,1},{4,2},{5,3},{6,4},{7,5},{0,6},{1,7},{10,8},{11,9},{12,... | collective-permute-start | bytes 1572872 | tf_op jit(solution)/shard_map/ppermute | solution.py:415

commit v7 on v6

--- a/solution.py
+++ b/solution.py
@@ -28,7 +28,7 @@
 def route_kernel(
     n_dev, cap, x_hbm, y_hbm, ids_hbm, slots_hbm, gates_hbm, w1_hbm, w2_hbm, w3_hbm,
     xr, zr, hb, dab, dbb, own_out, right_out, left_out,
-    xb, yb, mb, w1, w2, w3, w1t, w2t, w3t, dxb, oh, oht, gr, part, ddr, hopr, osum, ids, slots, gates,
+    xb, yb, mb, w1, w2, w3, w1t, w2t, w3t, dxb, oh, oht, gr, part, ddr, hopr, osum, lead, landed, ids, slots, gates,
     send_sem, recv_sem, load_sem,
 ):
     n_chip = n_dev // 2
@@ -169,12 +169,20 @@
         for e in range(n_loc):
             one(e, 0)
 
-    sums = (own_out, part.at[0], osum, part.at[1], right_out, part.at[2], left_out, part.at[3])
-
-    def combine(p, i, cols):
+    sums = (own_out, part.at[0], osum, part.at[1], None, part.at[2], None, part.at[3])
+
+    def outward(side, n):
+        if n == 0:
+            return lead.at[side]
+        return (right_out, left_out)[side].at[:, pl.ds((n - 1) * COLS, COLS)]
+
+    def combine(p, i, cols, n=None):
         q = FIRST[p] + i
         rows = jnp.concatenate([dxb[e, pl.ds(i * cap, cap), cols] for e in range(n_loc)], axis=0)
-        sums[q][:, cols] = dot(oht[q], rows)
+        if n is None:
+            sums[q][:, cols] = dot(oht[q], rows)
+        else:
+            outward(i // 2, n)[...] = dot(oht[q], rows)
 
     def forward(i):
         x_r[i].wait_recv()
@@ -287,10 +295,11 @@
         for c in hops[n]:
             c.wait_recv()
         near, far = pl.ds(0, half), pl.ds(half, half)
-        right_out[near, cols] += ddr[2, near, cols] + hopr[0, :, cols]
-        right_out[far, cols] += ddr[2, far, cols]
-        left_out[near, cols] += ddr[3, near, cols]
-        left_out[far, cols] += ddr[3, far, cols] + hopr[1, :, cols]
+        to_r, to_l = outward(0, n), outward(1, n)
+        to_r[near, :] += ddr[2, near, cols] + hopr[0, :, cols]
+        to_r[far, :] += ddr[2, far, cols]
+        to_l[near, :] += ddr[3, near, cols]
+        to_l[far, :] += ddr[3, far, cols] + hopr[1, :, cols]
 
     for n, cols in enumerate(chunks):
         back(2, cols)
@@ -299,14 +308,18 @@
         d_side.append((
             send(sums[5].at[:, cols], ddr.at[2, :, cols], mate),
             send(sums[7].at[:, cols], ddr.at[3, :, cols], mate)))
-        combine(2, 0, cols)
-        combine(2, 2, cols)
-        if n >= LAG:
-            side(n - LAG)
+        combine(2, 0, cols, n)
+        combine(2, 2, cols, n)
+        if n == 1:
+            side(0)
+            last = [send(lead.at[0], landed.at[0], right), send(lead.at[1], landed.at[1], left)]
     d_own.wait_recv()
     own_out[...] += ddr[0]
-    for n in range(n_cols - LAG, n_cols):
+    for n in range(1, n_cols):
         side(n)
+    for c in last:
+        c.wait_recv()
+    own_out[:, chunks[0]] += landed[0] + landed[1]
     for c in made:
         c.wait_send()
 
@@ -327,8 +340,8 @@
             jax.ShapeDtypeStruct((n_loc, n_rows, d_ff), BF),
             jax.ShapeDtypeStruct((n_loc, n_rows, d_ff), BF),
             jax.ShapeDtypeStruct((tok, d_model), F32),
-            jax.ShapeDtypeStruct((tok, d_model), F32),
-            jax.ShapeDtypeStruct((tok, d_model), F32),
+            jax.ShapeDtypeStruct((tok, d_model - COLS), F32),
+            jax.ShapeDtypeStruct((tok, d_model - COLS), F32),
         ),
         in_specs=[hbm] * 8,
         out_specs=[vmem] * 8,
@@ -350,6 +363,8 @@
             pltpu.VMEM((4, tok, d_model), F32),
             pltpu.VMEM((2, tok // 2, d_model), F32),
             pltpu.VMEM((tok, d_model), F32),
+            pltpu.VMEM((2, tok, COLS), F32),
+            pltpu.VMEM((2, tok, COLS), F32),
             pltpu.VMEM((top_k, tok), jnp.int32),
             pltpu.VMEM((top_k, tok), jnp.int32),
             pltpu.VMEM((top_k, tok), F32),
@@ -358,7 +373,7 @@
             pltpu.SemaphoreType.DMA((8,)),
         ],
         compiler_params=pltpu.CompilerParams(
-            collective_id=0, has_side_effects=True, vmem_limit_bytes=42000000),
+            collective_id=0, has_side_effects=True, vmem_limit_bytes=42400000),
         cost_estimate=pl.CostEstimate(flops=flops, bytes_accessed=14 * 1024 * 1024, transcendentals=0),
         name="route",
     )(*(pltpu.with_memory_space_constraint(v, pltpu.HBM) for v in (x, y, ids, slots, gates, w1, w2, w3)))
@@ -414,7 +429,7 @@
         from_left = lax.ppermute(right, "ep", to_right)
         from_right = lax.ppermute(left, "ep", to_left)
         g_gate, g_down, g_up = grads(xr, zr, h, da, db)
-        dx = (own + from_left + from_right).astype(BF)
+        dx = (own + jnp.pad(from_left + from_right, ((0, 0), (COLS, 0)))).astype(BF)
         return dx, g_gate, g_down, g_up
 
     tok_spec = P(("dp", "ep"), None)

time: 54.3 us -> 54.9 us (1.011)
  Pallas kernels: 48.5 us -> 50.6 us
  waiting for transfers between devices: 1.48 us -> 0.01 us
    pallas_call x1, Pallas kernels: 38 us -> 40.1 us  [route(): pl.pallas_call(functools.partial(route_kernel, n_dev, cap), out_shape=(ja...]
    ppermute x1, waiting for transfers between devices: 1.48 us -> 0.01 us  [local_step(): from_left = lax.ppermute(right, 'ep', to_right)]
    ppermute x1, starting transfers between devices: 0.11 us -> 0.72 us  [local_step(): from_left = lax.ppermute(right, 'ep', to_right)]
    ppermute x1, starting transfers between devices: 2.65 us -> 2.04 us  [local_step(): from_right = lax.ppermute(left, 'ep', to_left)]
  transfers between devices with their start and end apart: 2 -> 2, of which waited for: 1 -> 0; matrix products, arithmetic and copies ran while one was open for 0% -> 0% of each run, Pallas kernels for 19% -> 19%
where the time goes in v7:
time: 54.9 us; the launch traced here: 54.8 us
  Pallas kernels  50.6 us (92%)
  starting transfers between devices  2.76 us (5%)
  other arithmetic  0.81 us (1%)
  between operations  0.65 us (1%)
    pallas_call x1, Pallas kernels, route(): pl.pallas_call(functools.partial(route_kernel, n_dev, cap), out_shape=(ja...  40.1 us
    pallas_call x1, Pallas kernels, grads(): pl.pallas_call(grad_kernel, grid=(n_loc, parts), in_specs=[part(bm), full...  10.5 us
    ppermute x1, starting transfers between devices, local_step(): from_right = lax.ppermute(left, 'ep', to_left)  2.04 us
  transfers between devices with their start and end apart: 2, of which 0 were waited for; matrix products, arithmetic and copies ran while one was open for 0% of the time, Pallas kernels for 19%

profile of v7, /device:TPU:81, one launch (start us, length us, event | category | flops | bytes accessed | tf_op | source)
XLA Modules:
  0.0 54.8 jit_solution(7423562809175330834)
XLA Ops:
  0.6 40.1 %route.1 = (bf16[4,384,1024]{2,1,0:T(8,128)(2,1)S(1)}, bf16[4,384,1024]{2,1,0:T(8,128)(2,1)S(1)}, bf16[4,384,512]{2,1,0:T(8,128)(2,1)S(1)}, bf16[4,384,512]{2,1,...) custom-call(bf16[128,1024]{1,0:T(8,128)(2,1)} %x_hbm.1, ...), custom_call_target="tpu_custom_call" | custom-call | flops 8053063680 | bytes 14680064 | tf_op jit(solution)/shard_map/route/pallas_call | solution.py:334
  40.7 0.7 %collective-permute-start = (f32[128,768]{1,0:T(8,128)S(1)}, f32[128,768]{1,0:T(8,128)S(1)}, u32[]{:S(2)}, u32[]{:S(2)}) collective-permute-start(f32[128,768]{1,0:T(8,128)S(1)} %get-tuple-element.16), channel_id=1, source_target_pairs={{0,2},{1,3},{2,4},{3,5},{4,6},{5,7},{6,0},{7,1},{8,10},{9,11},{10,... | collective-permute-start | bytes 1179656 | tf_op jit(solution)/shard_map/ppermute | solution.py:429
  41.4 2.0 %collective-permute-start.1 = (f32[128,768]{1,0:T(8,128)S(1)}, f32[128,768]{1,0:T(8,128)S(1)}, u32[]{:S(2)}, u32[]{:S(2)}) collective-permute-start(f32[128,768]{1,0:T(8,128)S(1)} %get-tuple-element.17), channel_id=1, source_target_pairs={{2,0},{3,1},{4,2},{5,3},{6,4},{7,5},{0,6},{1,7},{10,8},{11,9},{12,... | collective-permute-start | bytes 1179656 | tf_op jit(solution)/shard_map/ppermute | solution.py:430
  43.5 10.5 %grads.1 = (f32[4,1024,512]{2,1,0:T(8,128)}, f32[4,512,1024]{2,1,0:T(8,128)}, f32[4,1024,512]{2,1,0:T(8,128)}) custom-call(bf16[4,384,1024]{2,1,0:T(8,128)(2,1)S(1)} %get-tuple-element.18.x_ref, bf16[4,384,1024]{2,1,0:T(8,128)(2,1)S(1)} %get-tuple-element.19.z_ref, bf16[4,384,512]{2,1,0:T(8,128)(2,1)S(1)} %get-tuple-element.20.h_ref, ...), custom_call_target="tpu_custom_call" | custom-call | flops 4831838208 | bytes 27262976 | tf_op jit(solution)/shard_map/grads/pallas_call | solution.py:395
  54.0 0.0 collective-permute-done
  54.0 0.0 collective-permute-done.1
  54.0 0.8 %add_convert_fusion = bf16[128,1024]{1,0:T(8,128)(2,1)} fusion(f32[128,1024]{1,0:T(8,128)S(1)} %get-tuple-element.15, f32[128,768]{1,0:T(8,128)S(1)} %add.8), kind=kLoop, calls=%fused_computation | loop fusion | flops 262144 | bytes 1179648 | tf_op jit(solution)/shard_map/convert_element_type | solution.py:432
  (1 shorter events, 0.0 us)
Async XLA Ops:
  40.7 13.2 %collective-permute-start = (f32[128,768]{1,0:T(8,128)S(1)}, f32[128,768]{1,0:T(8,128)S(1)}, u32[]{:S(2)}, u32[]{:S(2)}) collective-permute-start(f32[128,768]{1,0:T(8,128)S(1)} %get-tuple-element.16), channel_id=1, source_target_pairs={{0,2},{1,3},{2,4},{3,5},{4,6},{5,7},{6,0},{7,1},{8,10},{9,11},{10,... | collective-permute-start | bytes 1179656 | tf_op jit(solution)/shard_map/ppermute | solution.py:429
  41.4 12.5 %collective-permute-start.1 = (f32[128,768]{1,0:T(8,128)S(1)}, f32[128,768]{1,0:T(8,128)S(1)}, u32[]{:S(2)}, u32[]{:S(2)}) collective-permute-start(f32[128,768]{1,0:T(8,128)S(1)} %get-tuple-element.17), channel_id=1, source_target_pairs={{2,0},{3,1},{4,2},{5,3},{6,4},{7,5},{0,6},{1,7},{10,8},{11,9},{12,... | collective-permute-start | bytes 1179656 | tf_op jit(solution)/shard_map/ppermute | solution.py:430
